TPU v7x, 256 devices: a whole 4x4x8 slice. The times are simulated.
256 devices in a mesh: gx: 4 (over x), gy: 16 (over y, z_hi), gz: 4 (over z_lo, core).
Axes of the slice: x: 4, y: 4, z: 8 (z_hi: 4, z_lo: 2; z = z_hi * 2 + z_lo), core: 2. Of those that a mesh axis runs over, the one named last changes fastest.
Arguments:
- coef: float32 [4, 64, 512, 512], P(None, 'gx', 'gy', 'gz'), may hold values from -6 to 6
- keep: int32 [4, 16, 128, 128], P(None, 'gx', 'gy', 'gz'), may hold values from 1 to 10
- courant: float32 [64, 512, 512], P('gx', 'gy', 'gz'), may hold values from 0.05 to 0.2
- damp: float32 [64, 512, 512], P('gx', 'gy', 'gz'), may hold values from 0 to 0.3
- adj_next: float32 [64, 512, 512], P('gx', 'gy', 'gz'), may hold values from -6 to 6
- adj_now: float32 [64, 512, 512], P('gx', 'gy', 'gz'), may hold values from -6 to 6
- rec_cell: int32 [4, 16, 4, 128], P('gx', 'gy', 'gz'), may hold values from 0 to 65535
- rec_data: float32 [4, 16, 4, 4, 128], P('gx', 'gy', 'gz'), may hold values from -6 to 6
Outputs:
- gradient: float32 [64, 512, 512], P('gx', 'gy', 'gz')
- adjoint_last: float32 [64, 512, 512], P('gx', 'gy', 'gz')
- adjoint_before: float32 [64, 512, 512], P('gx', 'gy', 'gz')
Inputs may be any that keep to these rules, and one draw needn't show every extreme that they name: `keep`: A block's coefficient (a, b, c) is kept when a + b + c is below this count. `rec_cell`: A row-major index into the 16 x 32 x 128 cells of the device's own block; indices may repeat.
All inputs are finite; a program needn't handle non-finite values.
Results may differ from a plain program's by a relative error of at most 0.00013.
Values sent between devices are 32-bit elements; how exact they have to be, the bound alone decides.
A program may use at most 64 MiB of HBM per device.

v0:
```python
import jax
import jax.numpy as jnp
from jax import lax
from jax.sharding import PartitionSpec as P

STAR = (-205.0 / 72.0, 8.0 / 5.0, -1.0 / 5.0, 8.0 / 315.0, -1.0 / 560.0)


def with_halo(value, sides, width):
    edges = {}
    for axis, dim in sides:
        size, length = (lax.axis_size(axis), value.shape[dim])
        up = [(i, (i + 1) % size) for i in range(size - 1)]
        last = lax.slice_in_dim(value, length - width, length, axis=dim)
        leading = lax.slice_in_dim(value, 0, width, axis=dim)
        edges[dim] = (
            lax.ppermute(last, axis, up),
            lax.ppermute(leading, axis, [(b, a) for a, b in up]),
        )
    done = []
    for _, dim in sides:
        low, high = edges[dim]
        around = [(width, width) if d in done else (0, 0) for d in range(value.ndim)]
        value = jnp.concatenate([jnp.pad(low, around), value, jnp.pad(high, around)], axis=dim)
        done.append(dim)
    return value


def dct_table():
    freq = jnp.arange(4, dtype=jnp.float32)[:, None]
    place = jnp.arange(4, dtype=jnp.float32)[None, :]
    scales = jnp.where(freq == 0.0, 0.5, jnp.sqrt(jnp.float32(0.5)))
    return scales * jnp.cos(jnp.pi * (2.0 * place + 1.0) * freq / 8.0)


def block_table(length):
    return jnp.kron(jnp.eye(length // 4, dtype=jnp.float32), dct_table())


def decode(block_coef, block_keep):
    size_x, size_y, size_z = block_coef.shape
    levels = (
        (jnp.arange(size_x, dtype=jnp.int32) % 4)[:, None, None]
        + (jnp.arange(size_y, dtype=jnp.int32) % 4)[None, :, None]
        + (jnp.arange(size_z, dtype=jnp.int32) % 4)[None, None, :]
    )
    spread = jnp.repeat(jnp.repeat(jnp.repeat(block_keep, 4, axis=0), 4, axis=1), 4, axis=2)
    masked = jnp.where(levels < spread, block_coef, 0.0)
    along_z = jnp.dot(
        masked.reshape(size_x * size_y, size_z),
        block_table(size_z),
        precision=lax.Precision.HIGHEST,
    ).reshape(size_x, size_y, size_z)
    along_y = jnp.einsum(
        "bj,ibk->ijk", block_table(size_y), along_z, precision=lax.Precision.HIGHEST
    )
    along_x = jnp.dot(
        block_table(size_x).T,
        along_y.reshape(size_x, size_y * size_z),
        precision=lax.Precision.HIGHEST,
    )
    return along_x.reshape(size_x, size_y, size_z)


def star_padded(padded, shape):
    size_x, size_y, size_z = shape
    total = 3.0 * STAR[0] * padded[4 : 4 + size_x, 4 : 4 + size_y, 4 : 4 + size_z]
    for reach in range(1, 5):
        plus_x = padded[4 + reach : 4 + reach + size_x, 4 : 4 + size_y, 4 : 4 + size_z]
        minus_x = padded[4 - reach : 4 - reach + size_x, 4 : 4 + size_y, 4 : 4 + size_z]
        plus_y = padded[4 : 4 + size_x, 4 + reach : 4 + reach + size_y, 4 : 4 + size_z]
        minus_y = padded[4 : 4 + size_x, 4 - reach : 4 - reach + size_y, 4 : 4 + size_z]
        plus_z = padded[4 : 4 + size_x, 4 : 4 + size_y, 4 + reach : 4 + reach + size_z]
        minus_z = padded[4 : 4 + size_x, 4 : 4 + size_y, 4 - reach : 4 - reach + size_z]
        total = total + STAR[reach] * (plus_x + minus_x + plus_y + minus_y + plus_z + minus_z)
    return total


def adjoint_laplace(field):
    padded = with_halo(field, (("gx", 0), ("gy", 1), ("gz", 2)), 4)
    return star_padded(padded, field.shape)


def local(coef, keep, courant, damp, adj_next, adj_now, rec_cell, rec_data):
    shape = adj_now.shape
    cells = shape[0] * shape[1] * shape[2]
    forwards = [decode(coef[step], keep[step]) for step in range(coef.shape[0])]
    stacked = jnp.stack(forwards)
    padded_all = with_halo(stacked, (("gx", 1), ("gy", 2), ("gz", 3)), 4)
    positions = rec_cell.reshape(-1)
    gradient = jnp.zeros(shape, jnp.float32)
    later = adj_next
    current = adj_now
    for step in range(coef.shape[0]):
        forward_lap = star_padded(padded_all[step], shape)
        gradient = gradient + courant * current * forward_lap
        inject = (
            jnp.zeros((cells,), jnp.float32)
            .at[positions]
            .add(rec_data[0, 0, 0, step])
            .reshape(shape)
        )
        earlier = (
            2.0 * current - (1.0 - damp) * later + courant * adjoint_laplace(current) + inject
        ) / (1.0 + damp)
        later = current
        current = earlier
    return (gradient, current, later)


def solution(mesh):
    in_specs = (
        P(None, "gx", "gy", "gz"),
        P(None, "gx", "gy", "gz"),
        P("gx", "gy", "gz"),
        P("gx", "gy", "gz"),
        P("gx", "gy", "gz"),
        P("gx", "gy", "gz"),
        P("gx", "gy", "gz", None),
        P("gx", "gy", "gz", None, None),
    )
    out_specs = (P("gx", "gy", "gz"), P("gx", "gy", "gz"), P("gx", "gy", "gz"))
    return jax.shard_map(local, mesh=mesh, in_specs=in_specs, out_specs=out_specs, check_vma=False)
```

profile of v0, /device:TPU:62, one launch (start us, length us, event | category | flops | bytes accessed | tf_op | source)
XLA Modules:
  0.0 197.4 jit_solution(1952567716401919592)
XLA Ops:
  11.1 2.4 %copy.212 = f32[1,16,32,128]{2,1,3,0:T(8,128)} copy(f32[1,16,32,128]{3,2,1,0:T(8,128)} %get-tuple-element.29) | data formatting | bytes 524288
  28.0 2.0 %fusion.11 = f32[16,32,128]{2,1,0:T(8,128)S(1)} fusion(f32[128,128,1]{1,0,2:T(8,128)S(1)} %reshape.494, f32[16,32,128]{1,0,2:T(8,128)S(1)} %get-tuple-element.77), kind=kOutput, calls=%fused_computation.33 | convolution fusion | flops 100663296 | bytes 589824 | tf_op jit(solution)/shard_map/dot_general | solution.py:49
  32.8 2.4 %copy.172 = f32[4,16,32,4]{2,1,3,0:T(8,128)} copy(f32[4,16,32,4]{3,1,2,0:T(8,128)} %get-tuple-element.24) | data formatting | bytes 65536 | tf_op jit(solution)/shard_map/slice | solution.py:15
  39.2 7.9 %collective-permute-start.8 = (f32[16,4,128]{2,0,1:T(8,128)S(1)}, f32[16,4,128]{2,0,1:T(8,128)S(1)}, u32[]{:S(2)}, u32[]{:S(2)}) collective-permute-start(f32[16,4,128]{2,0,1:T(8,128)S(1)} %get-tuple-element.70), channel_id=1, source_target_pairs={{4,0},{8,4},{12,8},{16,12},{20,16},{24,20},{28,24},{32,28},{36,32}... | collective-permute-start | bytes 98312 | tf_op jit(solution)/shard_map/ppermute | solution.py:18
  47.1 4.5 %collective-permute-start.6 = (f32[4,32,128]{2,0,1:T(4,128)S(1)}, f32[4,32,128]{2,0,1:T(4,128)S(1)}, u32[]{:S(2)}, u32[]{:S(2)}) collective-permute-start(f32[4,32,128]{2,0,1:T(4,128)S(1)} %get-tuple-element.71), channel_id=1, source_target_pairs={{64,0},{128,64},{192,128},{65,1},{129,65},{193,129},{66,2},{130,66... | collective-permute-start | bytes 196616 | tf_op jit(solution)/shard_map/ppermute | solution.py:18
  51.7 1.9 collective-permute-start.9
  55.4 2.4 %copy.170 = f32[4,16,32,4]{2,1,3,0:T(8,128)} copy(f32[4,16,32,4]{3,1,2,0:T(8,128)} %get-tuple-element.23) | data formatting | bytes 65536 | tf_op jit(solution)/shard_map/slice | solution.py:14
  62.4 2.4 %collective-permute-start.11 = (f32[16,32,4]{2,0,1:T(8,128)}, f32[16,32,4]{2,0,1:T(8,128)S(1)}, u32[]{:S(2)}, u32[]{:S(2)}) collective-permute-start(f32[16,32,4]{2,0,1:T(8,128)} %get-tuple-element.68), channel_id=1, source_target_pairs={{0,1},{1,2},{2,3},{4,5},{5,6},{6,7},{8,9},{9,10},{10,11},{12,13},{... | collective-permute-start | bytes 24584 | tf_op jit(solution)/shard_map/ppermute | solution.py:17
  66.6 3.7 %collective-permute-done.11 = f32[16,32,4]{2,0,1:T(8,128)S(1)} collective-permute-done((f32[16,32,4]{2,0,1:T(8,128)}, f32[16,32,4]{2,0,1:T(8,128)S(1)}, u32[]{:S(2)}, u32[]{:S(2)}) %collective-permute-start.11) | collective-permute-done | bytes 8224 | tf_op jit(solution)/shard_map/ppermute | solution.py:17
  70.8 2.3 %fusion.121 = f32[16,32,128]{2,0,1:T(8,128)S(1)} fusion(f32[16,32,128]{2,0,1:T(8,128)S(1)} %get-tuple-element.66, f32[4,32,128]{2,0,1:T(4,128)S(1)} %collective-permute-done.7, f32[24,40,132]{2,0,1:T(8,128)S(1)} %get-tuple-element.38, f32[24,40,132]{2,0,1:T(8,128)S(1)} %get-tuple-element.37, f32[24,36,128]{2,0,1:T(8,128)S(1)} %get-tuple-element.46, ...), kind=kLoop, calls=%fused_computation.212 | loop fusion | flops 2752512 | bytes 6881280 | tf_op jit(solution)/shard_map/div | solution.py:103
  74.4 4.5 %collective-permute-start.12 = (f32[4,32,128]{2,0,1:T(4,128)S(1)}, f32[4,32,128]{2,0,1:T(4,128)S(1)}, u32[]{:S(2)}, u32[]{:S(2)}) collective-permute-start(f32[4,32,128]{2,0,1:T(4,128)S(1)} %get-tuple-element.63), channel_id=1, source_target_pairs={{64,0},{128,64},{192,128},{65,1},{129,65},{193,129},{66,2},{130,66... | collective-permute-start | bytes 196616 | tf_op jit(solution)/shard_map/ppermute | solution.py:18
  79.0 6.9 %collective-permute-start.14 = (f32[16,4,128]{2,0,1:T(8,128)S(1)}, f32[16,4,128]{2,0,1:T(8,128)S(1)}, u32[]{:S(2)}, u32[]{:S(2)}) collective-permute-start(f32[16,4,128]{2,0,1:T(8,128)S(1)} %get-tuple-element.62), channel_id=1, source_target_pairs={{4,0},{8,4},{12,8},{16,12},{20,16},{24,20},{28,24},{32,28},{36,32}... | collective-permute-start | bytes 98312 | tf_op jit(solution)/shard_map/ppermute | solution.py:18
  85.9 1.9 collective-permute-start.15
  88.0 1.9 collective-permute-start
  90.0 4.8 %collective-permute-done.15 = f32[16,4,128]{2,0,1:T(8,128)S(1)} collective-permute-done((f32[16,4,128]{2,0,1:T(8,128)S(1)}, f32[16,4,128]{2,0,1:T(8,128)S(1)}, u32[]{:S(2)}, u32[]{:S(2)}) %collective-permute-start.15) | collective-permute-done | bytes 32800 | tf_op jit(solution)/shard_map/ppermute | solution.py:17
  96.7 2.4 %collective-permute-start.17 = (f32[16,32,4]{2,0,1:T(8,128)S(1)}, f32[16,32,4]{2,0,1:T(8,128)S(1)}, u32[]{:S(2)}, u32[]{:S(2)}) collective-permute-start(f32[16,32,4]{2,0,1:T(8,128)S(1)} %get-tuple-element.60), channel_id=1, source_target_pairs={{0,1},{1,2},{2,3},{4,5},{5,6},{6,7},{8,9},{9,10},{10,11},{12,13},{... | collective-permute-start | bytes 24584 | tf_op jit(solution)/shard_map/ppermute | solution.py:17
  100.5 3.8 %collective-permute-done.17 = f32[16,32,4]{2,0,1:T(8,128)S(1)} collective-permute-done((f32[16,32,4]{2,0,1:T(8,128)S(1)}, f32[16,32,4]{2,0,1:T(8,128)S(1)}, u32[]{:S(2)}, u32[]{:S(2)}) %collective-permute-start.17) | collective-permute-done | bytes 8224 | tf_op jit(solution)/shard_map/ppermute | solution.py:17
  107.7 3.9 %collective-permute-start.20 = (f32[16,4,128]{2,0,1:T(8,128)S(1)}, f32[16,4,128]{2,0,1:T(8,128)S(1)}, u32[]{:S(2)}, u32[]{:S(2)}) collective-permute-start(f32[16,4,128]{2,0,1:T(8,128)S(1)} %get-tuple-element.56), channel_id=1, source_target_pairs={{4,0},{8,4},{12,8},{16,12},{20,16},{24,20},{28,24},{32,28},{36,32}... | collective-permute-start | bytes 98312 | tf_op jit(solution)/shard_map/ppermute | solution.py:18
  114.2 2.7 %collective-permute-start.18 = (f32[4,32,128]{2,0,1:T(4,128)}, f32[4,32,128]{2,0,1:T(4,128)S(1)}, u32[]{:S(2)}, u32[]{:S(2)}) collective-permute-start(f32[4,32,128]{2,0,1:T(4,128)} %get-tuple-element.58), channel_id=1, source_target_pairs={{64,0},{128,64},{192,128},{65,1},{129,65},{193,129},{66,2},{130,66... | collective-permute-start | bytes 196616 | tf_op jit(solution)/shard_map/ppermute | solution.py:18
  118.2 2.9 %collective-permute-start.21 = (f32[16,4,128]{2,0,1:T(8,128)}, f32[16,4,128]{2,0,1:T(8,128)}, u32[]{:S(2)}, u32[]{:S(2)}) collective-permute-start(f32[16,4,128]{2,0,1:T(8,128)} %get-tuple-element.55), channel_id=1, source_target_pairs={{0,4},{4,8},{8,12},{12,16},{16,20},{20,24},{24,28},{28,32},{32,36}... | collective-permute-start | bytes 98312 | tf_op jit(solution)/shard_map/ppermute | solution.py:17
  121.1 2.5 %collective-permute-start.23 = (f32[16,32,4]{2,0,1:T(8,128)}, f32[16,32,4]{2,0,1:T(8,128)}, u32[]{:S(2)}, u32[]{:S(2)}) collective-permute-start(f32[16,32,4]{2,0,1:T(8,128)} %get-tuple-element.54), channel_id=1, source_target_pairs={{0,1},{1,2},{2,3},{4,5},{5,6},{6,7},{8,9},{9,10},{10,11},{12,13},{... | collective-permute-start | bytes 24584 | tf_op jit(solution)/shard_map/ppermute | solution.py:17
  124.4 1.9 scatter_custom_fusion.2
  131.1 6.0 %collective-permute-start.4 = (f32[4,16,4,128]{3,1,2,0:T(8,128)}, f32[4,16,4,128]{3,1,2,0:T(8,128)S(1)}, u32[]{:S(2)}, u32[]{:S(2)}) collective-permute-start(f32[4,16,4,128]{3,1,2,0:T(8,128)} %get-tuple-element.26), channel_id=1, source_target_pairs={{4,0},{8,4},{12,8},{16,12},{20,16},{24,20},{28,24},{32,28},{36,32}... | collective-permute-start | bytes 393224 | tf_op jit(solution)/shard_map/ppermute | solution.py:18
  139.8 4.3 %collective-permute-start.3 = (f32[4,4,32,128]{3,1,2,0:T(4,128)}, f32[4,4,32,128]{3,1,2,0:T(4,128)S(1)}, u32[]{:S(2)}, u32[]{:S(2)}) collective-permute-start(f32[4,4,32,128]{3,1,2,0:T(4,128)} %get-tuple-element.22), channel_id=1, source_target_pairs={{64,0},{128,64},{192,128},{65,1},{129,65},{193,129},{66,2},{130,66... | collective-permute-start | bytes 786440 | tf_op jit(solution)/shard_map/ppermute | solution.py:18
  149.2 4.0 %collective-permute-done.2 = f32[4,4,32,128]{3,1,2,0:T(4,128)S(1)} collective-permute-done((f32[4,4,32,128]{3,1,2,0:T(4,128)}, f32[4,4,32,128]{3,1,2,0:T(4,128)S(1)}, u32[]{:S(2)}, u32[]{:S(2)}) %collective-permute-start.2) | collective-permute-done | bytes 262176 | tf_op jit(solution)/shard_map/ppermute | solution.py:17
  153.3 6.9 %select_maximum_fusion = f32[4,24,40,136]{3,1,2,0:T(8,128)S(1)} fusion(f32[4,16,32,4]{3,1,2,0:T(8,128)S(1)} %copy.173, f32[4,16,4,128]{3,1,2,0:T(8,128)S(1)} %collective-permute-done.4, f32[4,16,4,128]{3,1,2,0:T(8,128)S(1)} %collective-permute-done.1, f32[4,16,32,4]{3,1,2,0:T(8,128)S(1)} %copy.171, f32[4,4,32,128]{3,1,2,0:T(4,128)S(1)} %collective-permute-done.3, ...), kind=kLoop, calls=%fused_computation.10 | loop fusion | flops 13056000 | bytes 3989504 | tf_op jit(solution)/shard_map/concatenate | solution.py:24
  161.3 7.7 %fusion.151 = (f32[16,32,128]{2,0,1:T(8,128)S(1)}, f32[16,32,128]{2,0,1:T(8,128)S(1)}) fusion(f32[24,40,136]{2,0,1:T(8,128)S(1)} %get-tuple-element.18, f32[24,40,136]{2,0,1:T(8,128)S(1)} %get-tuple-element.19, f32[24,40,136]{2,0,1:T(8,128)S(1)} %get-tuple-element.20, f32[24,40,136]{2,0,1:T(8,128)S(1)} %get-tuple-element.17, f32[16,32,128]{2,0,1:T(8,128)S(1)} %fusion.89, ...), kind=kLoop, calls=%fused_computation.253 | loop fusion | flops 11337728 | bytes 32636928 | tf_op jit(solution)/shard_map/add | solution.py:96
  170.4 4.5 %collective-permute-start.24 = (f32[4,32,128]{2,0,1:T(4,128)S(1)}, f32[4,32,128]{2,0,1:T(4,128)S(1)}, u32[]{:S(2)}, u32[]{:S(2)}) collective-permute-start(f32[4,32,128]{2,0,1:T(4,128)S(1)} %get-tuple-element.51), channel_id=1, source_target_pairs={{64,0},{128,64},{192,128},{65,1},{129,65},{193,129},{66,2},{130,66... | collective-permute-start | bytes 196616 | tf_op jit(solution)/shard_map/ppermute | solution.py:18
  175.0 6.7 %collective-permute-start.26 = (f32[16,4,128]{2,0,1:T(8,128)S(1)}, f32[16,4,128]{2,0,1:T(8,128)S(1)}, u32[]{:S(2)}, u32[]{:S(2)}) collective-permute-start(f32[16,4,128]{2,0,1:T(8,128)S(1)} %get-tuple-element.50), channel_id=1, source_target_pairs={{4,0},{8,4},{12,8},{16,12},{20,16},{24,20},{28,24},{32,28},{36,32}... | collective-permute-start | bytes 98312 | tf_op jit(solution)/shard_map/ppermute | solution.py:18
  181.7 1.9 collective-permute-start.27
  187.2 2.4 %collective-permute-start.29 = (f32[16,32,4]{2,0,1:T(8,128)S(1)}, f32[16,32,4]{2,0,1:T(8,128)S(1)}, u32[]{:S(2)}, u32[]{:S(2)}) collective-permute-start(f32[16,32,4]{2,0,1:T(8,128)S(1)} %get-tuple-element.48), channel_id=1, source_target_pairs={{0,1},{1,2},{2,3},{4,5},{5,6},{6,7},{8,9},{9,10},{10,11},{12,13},{... | collective-permute-start | bytes 24584 | tf_op jit(solution)/shard_map/ppermute | solution.py:17
  191.1 3.8 %collective-permute-done.29 = f32[16,32,4]{2,0,1:T(8,128)S(1)} collective-permute-done((f32[16,32,4]{2,0,1:T(8,128)S(1)}, f32[16,32,4]{2,0,1:T(8,128)S(1)}, u32[]{:S(2)}, u32[]{:S(2)}) %collective-permute-start.29) | collective-permute-done | bytes 8224 | tf_op jit(solution)/shard_map/ppermute | solution.py:17
  (174 shorter events, 75.1 us)
Async XLA Ops:
  24.7 98.9 %copy-start.2 = (f32[1,16,32,128]{3,1,2,0:T(8,128)}, f32[1,16,32,128]{3,1,2,0:T(8,128)S(1)}, u32[]{:S(2)}) copy-start(f32[1,16,32,128]{3,1,2,0:T(8,128)S(1)} %convolution_bitcast_fusion) | copy-start | bytes 786436
  25.2 98.4 %copy-start.4 = (f32[1,16,32,128]{3,1,2,0:T(8,128)}, f32[1,16,32,128]{3,1,2,0:T(8,128)S(1)}, u32[]{:S(2)}) copy-start(f32[1,16,32,128]{3,1,2,0:T(8,128)S(1)} %convolution_bitcast_fusion.1) | copy-start | bytes 786436
  35.2 81.7 %collective-permute-start.5 = (f32[4,16,32,4]{2,1,3,0:T(8,128)}, f32[4,16,32,4]{2,1,3,0:T(8,128)S(1)}, u32[]{:S(2)}, u32[]{:S(2)}) collective-permute-start(f32[4,16,32,4]{2,1,3,0:T(8,128)} %copy.172), channel_id=1, source_target_pairs={{1,0},{2,1},{3,2},{5,4},{6,5},{7,6},{9,8},{10,9},{11,10},{13,12},{... | collective-permute-start | bytes 98312 | tf_op jit(solution)/shard_map/ppermute | solution.py:18
  37.3 27.5 %collective-permute-start.7 = (f32[4,32,128]{2,0,1:T(4,128)S(1)}, f32[4,32,128]{2,0,1:T(4,128)S(1)}, u32[]{:S(2)}, u32[]{:S(2)}) collective-permute-start(f32[4,32,128]{2,0,1:T(4,128)S(1)} %get-tuple-element.72), channel_id=1, source_target_pairs={{0,64},{64,128},{128,192},{1,65},{65,129},{129,193},{2,66},{66,130... | collective-permute-start | bytes 196616 | tf_op jit(solution)/shard_map/ppermute | solution.py:17
  39.2 21.2 %collective-permute-start.8 = (f32[16,4,128]{2,0,1:T(8,128)S(1)}, f32[16,4,128]{2,0,1:T(8,128)S(1)}, u32[]{:S(2)}, u32[]{:S(2)}) collective-permute-start(f32[16,4,128]{2,0,1:T(8,128)S(1)} %get-tuple-element.70), channel_id=1, source_target_pairs={{4,0},{8,4},{12,8},{16,12},{20,16},{24,20},{28,24},{32,28},{36,32}... | collective-permute-start | bytes 98312 | tf_op jit(solution)/shard_map/ppermute | solution.py:18
  47.1 17.7 %collective-permute-start.6 = (f32[4,32,128]{2,0,1:T(4,128)S(1)}, f32[4,32,128]{2,0,1:T(4,128)S(1)}, u32[]{:S(2)}, u32[]{:S(2)}) collective-permute-start(f32[4,32,128]{2,0,1:T(4,128)S(1)} %get-tuple-element.71), channel_id=1, source_target_pairs={{64,0},{128,64},{192,128},{65,1},{129,65},{193,129},{66,2},{130,66... | collective-permute-start | bytes 196616 | tf_op jit(solution)/shard_map/ppermute | solution.py:18
  51.7 10.7 %collective-permute-start.9 = (f32[16,4,128]{2,0,1:T(8,128)}, f32[16,4,128]{2,0,1:T(8,128)S(1)}, u32[]{:S(2)}, u32[]{:S(2)}) collective-permute-start(f32[16,4,128]{2,0,1:T(8,128)} %get-tuple-element.69), channel_id=1, source_target_pairs={{0,4},{4,8},{8,12},{12,16},{16,20},{20,24},{24,28},{28,32},{32,36}... | collective-permute-start | bytes 98312 | tf_op jit(solution)/shard_map/ppermute | solution.py:17
  60.4 6.1 %collective-permute-start.10 = (f32[16,32,4]{2,0,1:T(8,128)}, f32[16,32,4]{2,0,1:T(8,128)S(1)}, u32[]{:S(2)}, u32[]{:S(2)}) collective-permute-start(f32[16,32,4]{2,0,1:T(8,128)} %get-tuple-element.67), channel_id=1, source_target_pairs={{1,0},{2,1},{3,2},{5,4},{6,5},{7,6},{9,8},{10,9},{11,10},{13,12},{... | collective-permute-start | bytes 24584 | tf_op jit(solution)/shard_map/ppermute | solution.py:18
  62.4 7.9 %collective-permute-start.11 = (f32[16,32,4]{2,0,1:T(8,128)}, f32[16,32,4]{2,0,1:T(8,128)S(1)}, u32[]{:S(2)}, u32[]{:S(2)}) collective-permute-start(f32[16,32,4]{2,0,1:T(8,128)} %get-tuple-element.68), channel_id=1, source_target_pairs={{0,1},{1,2},{2,3},{4,5},{5,6},{6,7},{8,9},{9,10},{10,11},{12,13},{... | collective-permute-start | bytes 24584 | tf_op jit(solution)/shard_map/ppermute | solution.py:17
  73.1 23.5 %collective-permute-start.13 = (f32[4,32,128]{2,0,1:T(4,128)S(1)}, f32[4,32,128]{2,0,1:T(4,128)S(1)}, u32[]{:S(2)}, u32[]{:S(2)}) collective-permute-start(f32[4,32,128]{2,0,1:T(4,128)S(1)} %get-tuple-element.64), channel_id=1, source_target_pairs={{0,64},{64,128},{128,192},{1,65},{65,129},{129,193},{2,66},{66,130... | collective-permute-start | bytes 196616 | tf_op jit(solution)/shard_map/ppermute | solution.py:17
  74.4 24.7 %collective-permute-start.12 = (f32[4,32,128]{2,0,1:T(4,128)S(1)}, f32[4,32,128]{2,0,1:T(4,128)S(1)}, u32[]{:S(2)}, u32[]{:S(2)}) collective-permute-start(f32[4,32,128]{2,0,1:T(4,128)S(1)} %get-tuple-element.63), channel_id=1, source_target_pairs={{64,0},{128,64},{192,128},{65,1},{129,65},{193,129},{66,2},{130,66... | collective-permute-start | bytes 196616 | tf_op jit(solution)/shard_map/ppermute | solution.py:18
  79.0 9.0 %collective-permute-start.14 = (f32[16,4,128]{2,0,1:T(8,128)S(1)}, f32[16,4,128]{2,0,1:T(8,128)S(1)}, u32[]{:S(2)}, u32[]{:S(2)}) collective-permute-start(f32[16,4,128]{2,0,1:T(8,128)S(1)} %get-tuple-element.62), channel_id=1, source_target_pairs={{4,0},{8,4},{12,8},{16,12},{20,16},{24,20},{28,24},{32,28},{36,32}... | collective-permute-start | bytes 98312 | tf_op jit(solution)/shard_map/ppermute | solution.py:18
  85.9 8.8 %collective-permute-start.15 = (f32[16,4,128]{2,0,1:T(8,128)S(1)}, f32[16,4,128]{2,0,1:T(8,128)S(1)}, u32[]{:S(2)}, u32[]{:S(2)}) collective-permute-start(f32[16,4,128]{2,0,1:T(8,128)S(1)} %get-tuple-element.61), channel_id=1, source_target_pairs={{0,4},{4,8},{8,12},{12,16},{16,20},{20,24},{24,28},{28,32},{32,36}... | collective-permute-start | bytes 98312 | tf_op jit(solution)/shard_map/ppermute | solution.py:17
  88.0 30.2 %collective-permute-start = (f32[4,16,32,4]{2,1,3,0:T(8,128)S(1)}, f32[4,16,32,4]{2,1,3,0:T(8,128)S(1)}, u32[]{:S(2)}, u32[]{:S(2)}) collective-permute-start(f32[4,16,32,4]{2,1,3,0:T(8,128)S(1)} %copy-done.15), channel_id=1, source_target_pairs={{0,1},{1,2},{2,3},{4,5},{5,6},{6,7},{8,9},{9,10},{10,11},{12,13},{... | collective-permute-start | bytes 98312 | tf_op jit(solution)/shard_map/ppermute | solution.py:17
  94.7 5.8 %collective-permute-start.16 = (f32[16,32,4]{2,0,1:T(8,128)S(1)}, f32[16,32,4]{2,0,1:T(8,128)S(1)}, u32[]{:S(2)}, u32[]{:S(2)}) collective-permute-start(f32[16,32,4]{2,0,1:T(8,128)S(1)} %get-tuple-element.59), channel_id=1, source_target_pairs={{1,0},{2,1},{3,2},{5,4},{6,5},{7,6},{9,8},{10,9},{11,10},{13,12},{... | collective-permute-start | bytes 24584 | tf_op jit(solution)/shard_map/ppermute | solution.py:18
  96.7 7.7 %collective-permute-start.17 = (f32[16,32,4]{2,0,1:T(8,128)S(1)}, f32[16,32,4]{2,0,1:T(8,128)S(1)}, u32[]{:S(2)}, u32[]{:S(2)}) collective-permute-start(f32[16,32,4]{2,0,1:T(8,128)S(1)} %get-tuple-element.60), channel_id=1, source_target_pairs={{0,1},{1,2},{2,3},{4,5},{5,6},{6,7},{8,9},{9,10},{10,11},{12,13},{... | collective-permute-start | bytes 24584 | tf_op jit(solution)/shard_map/ppermute | solution.py:17
  107.7 13.4 %collective-permute-start.20 = (f32[16,4,128]{2,0,1:T(8,128)S(1)}, f32[16,4,128]{2,0,1:T(8,128)S(1)}, u32[]{:S(2)}, u32[]{:S(2)}) collective-permute-start(f32[16,4,128]{2,0,1:T(8,128)S(1)} %get-tuple-element.56), channel_id=1, source_target_pairs={{4,0},{8,4},{12,8},{16,12},{20,16},{24,20},{28,24},{32,28},{36,32}... | collective-permute-start | bytes 98312 | tf_op jit(solution)/shard_map/ppermute | solution.py:18
  112.3 25.7 %collective-permute-start.22 = (f32[16,32,4]{2,0,1:T(8,128)}, f32[16,32,4]{2,0,1:T(8,128)}, u32[]{:S(2)}, u32[]{:S(2)}) collective-permute-start(f32[16,32,4]{2,0,1:T(8,128)} %get-tuple-element.53), channel_id=1, source_target_pairs={{1,0},{2,1},{3,2},{5,4},{6,5},{7,6},{9,8},{10,9},{11,10},{13,12},{... | collective-permute-start | bytes 24584 | tf_op jit(solution)/shard_map/ppermute | solution.py:18
  114.2 30.0 %collective-permute-start.18 = (f32[4,32,128]{2,0,1:T(4,128)}, f32[4,32,128]{2,0,1:T(4,128)S(1)}, u32[]{:S(2)}, u32[]{:S(2)}) collective-permute-start(f32[4,32,128]{2,0,1:T(4,128)} %get-tuple-element.58), channel_id=1, source_target_pairs={{64,0},{128,64},{192,128},{65,1},{129,65},{193,129},{66,2},{130,66... | collective-permute-start | bytes 196616 | tf_op jit(solution)/shard_map/ppermute | solution.py:18
  116.9 28.5 %collective-permute-start.19 = (f32[4,32,128]{2,0,1:T(4,128)}, f32[4,32,128]{2,0,1:T(4,128)S(1)}, u32[]{:S(2)}, u32[]{:S(2)}) collective-permute-start(f32[4,32,128]{2,0,1:T(4,128)} %get-tuple-element.57), channel_id=1, source_target_pairs={{0,64},{64,128},{128,192},{1,65},{65,129},{129,193},{2,66},{66,130... | collective-permute-start | bytes 196616 | tf_op jit(solution)/shard_map/ppermute | solution.py:17
  118.2 12.9 %collective-permute-start.21 = (f32[16,4,128]{2,0,1:T(8,128)}, f32[16,4,128]{2,0,1:T(8,128)}, u32[]{:S(2)}, u32[]{:S(2)}) collective-permute-start(f32[16,4,128]{2,0,1:T(8,128)} %get-tuple-element.55), channel_id=1, source_target_pairs={{0,4},{4,8},{8,12},{12,16},{16,20},{20,24},{24,28},{28,32},{32,36}... | collective-permute-start | bytes 98312 | tf_op jit(solution)/shard_map/ppermute | solution.py:17
  121.1 18.7 %collective-permute-start.23 = (f32[16,32,4]{2,0,1:T(8,128)}, f32[16,32,4]{2,0,1:T(8,128)}, u32[]{:S(2)}, u32[]{:S(2)}) collective-permute-start(f32[16,32,4]{2,0,1:T(8,128)} %get-tuple-element.54), channel_id=1, source_target_pairs={{0,1},{1,2},{2,3},{4,5},{5,6},{6,7},{8,9},{9,10},{10,11},{12,13},{... | collective-permute-start | bytes 24584 | tf_op jit(solution)/shard_map/ppermute | solution.py:17
  131.1 15.9 %collective-permute-start.4 = (f32[4,16,4,128]{3,1,2,0:T(8,128)}, f32[4,16,4,128]{3,1,2,0:T(8,128)S(1)}, u32[]{:S(2)}, u32[]{:S(2)}) collective-permute-start(f32[4,16,4,128]{3,1,2,0:T(8,128)} %get-tuple-element.26), channel_id=1, source_target_pairs={{4,0},{8,4},{12,8},{16,12},{20,16},{24,20},{28,24},{32,28},{36,32}... | collective-permute-start | bytes 393224 | tf_op jit(solution)/shard_map/ppermute | solution.py:18
  137.9 10.2 %collective-permute-start.1 = (f32[4,16,4,128]{3,1,2,0:T(8,128)}, f32[4,16,4,128]{3,1,2,0:T(8,128)S(1)}, u32[]{:S(2)}, u32[]{:S(2)}) collective-permute-start(f32[4,16,4,128]{3,1,2,0:T(8,128)} %get-tuple-element.25), channel_id=1, source_target_pairs={{0,4},{4,8},{8,12},{12,16},{16,20},{20,24},{24,28},{28,32},{32,36}... | collective-permute-start | bytes 393224 | tf_op jit(solution)/shard_map/ppermute | solution.py:17
  139.8 9.4 %collective-permute-start.3 = (f32[4,4,32,128]{3,1,2,0:T(4,128)}, f32[4,4,32,128]{3,1,2,0:T(4,128)S(1)}, u32[]{:S(2)}, u32[]{:S(2)}) collective-permute-start(f32[4,4,32,128]{3,1,2,0:T(4,128)} %get-tuple-element.22), channel_id=1, source_target_pairs={{64,0},{128,64},{192,128},{65,1},{129,65},{193,129},{66,2},{130,66... | collective-permute-start | bytes 786440 | tf_op jit(solution)/shard_map/ppermute | solution.py:18
  144.1 9.1 %collective-permute-start.2 = (f32[4,4,32,128]{3,1,2,0:T(4,128)}, f32[4,4,32,128]{3,1,2,0:T(4,128)S(1)}, u32[]{:S(2)}, u32[]{:S(2)}) collective-permute-start(f32[4,4,32,128]{3,1,2,0:T(4,128)} %get-tuple-element.21), channel_id=1, source_target_pairs={{0,64},{64,128},{128,192},{1,65},{65,129},{129,193},{2,66},{66,130... | collective-permute-start | bytes 786440 | tf_op jit(solution)/shard_map/ppermute | solution.py:17
  169.0 21.5 %collective-permute-start.25 = (f32[4,32,128]{2,0,1:T(4,128)S(1)}, f32[4,32,128]{2,0,1:T(4,128)S(1)}, u32[]{:S(2)}, u32[]{:S(2)}) collective-permute-start(f32[4,32,128]{2,0,1:T(4,128)S(1)} %get-tuple-element.52), channel_id=1, source_target_pairs={{0,64},{64,128},{128,192},{1,65},{65,129},{129,193},{2,66},{66,130... | collective-permute-start | bytes 196616 | tf_op jit(solution)/shard_map/ppermute | solution.py:17
  170.4 20.0 %collective-permute-start.24 = (f32[4,32,128]{2,0,1:T(4,128)S(1)}, f32[4,32,128]{2,0,1:T(4,128)S(1)}, u32[]{:S(2)}, u32[]{:S(2)}) collective-permute-start(f32[4,32,128]{2,0,1:T(4,128)S(1)} %get-tuple-element.51), channel_id=1, source_target_pairs={{64,0},{128,64},{192,128},{65,1},{129,65},{193,129},{66,2},{130,66... | collective-permute-start | bytes 196616 | tf_op jit(solution)/shard_map/ppermute | solution.py:18
  175.0 12.2 %collective-permute-start.26 = (f32[16,4,128]{2,0,1:T(8,128)S(1)}, f32[16,4,128]{2,0,1:T(8,128)S(1)}, u32[]{:S(2)}, u32[]{:S(2)}) collective-permute-start(f32[16,4,128]{2,0,1:T(8,128)S(1)} %get-tuple-element.50), channel_id=1, source_target_pairs={{4,0},{8,4},{12,8},{16,12},{20,16},{24,20},{28,24},{32,28},{36,32}... | collective-permute-start | bytes 98312 | tf_op jit(solution)/shard_map/ppermute | solution.py:18
  181.7 8.8 %collective-permute-start.27 = (f32[16,4,128]{2,0,1:T(8,128)S(1)}, f32[16,4,128]{2,0,1:T(8,128)S(1)}, u32[]{:S(2)}, u32[]{:S(2)}) collective-permute-start(f32[16,4,128]{2,0,1:T(8,128)S(1)} %get-tuple-element.49), channel_id=1, source_target_pairs={{0,4},{4,8},{8,12},{12,16},{16,20},{20,24},{24,28},{28,32},{32,36}... | collective-permute-start | bytes 98312 | tf_op jit(solution)/shard_map/ppermute | solution.py:17
  185.3 5.8 %collective-permute-start.28 = (f32[16,32,4]{2,0,1:T(8,128)S(1)}, f32[16,32,4]{2,0,1:T(8,128)S(1)}, u32[]{:S(2)}, u32[]{:S(2)}) collective-permute-start(f32[16,32,4]{2,0,1:T(8,128)S(1)} %get-tuple-element.47), channel_id=1, source_target_pairs={{1,0},{2,1},{3,2},{5,4},{6,5},{7,6},{9,8},{10,9},{11,10},{13,12},{... | collective-permute-start | bytes 24584 | tf_op jit(solution)/shard_map/ppermute | solution.py:18
  187.2 7.7 %collective-permute-start.29 = (f32[16,32,4]{2,0,1:T(8,128)S(1)}, f32[16,32,4]{2,0,1:T(8,128)S(1)}, u32[]{:S(2)}, u32[]{:S(2)}) collective-permute-start(f32[16,32,4]{2,0,1:T(8,128)S(1)} %get-tuple-element.48), channel_id=1, source_target_pairs={{0,1},{1,2},{2,3},{4,5},{5,6},{6,7},{8,9},{9,10},{10,11},{12,13},{... | collective-permute-start | bytes 24584 | tf_op jit(solution)/shard_map/ppermute | solution.py:17
  (19 other events, 434.8 us)
where the time goes:
time: 199 us; the launch traced here: 197 us
  starting transfers between devices  90.4 us (45%)
  local copies, waits for them, and re-layouts  34.3 us (17%)
  other arithmetic  33 us (17%)
  waiting for transfers between devices  26.7 us (13%)
  matrix products  11.2 us (6%)
    ppermute x15, starting transfers between devices, with_halo(): lax.ppermute(leading, axis, [(b, a) for a, b in up])  61.6 us
    ppermute x15, starting transfers between devices, with_halo(): lax.ppermute(last, axis, up)  28.8 us
    ppermute x15, waiting for transfers between devices, with_halo(): lax.ppermute(last, axis, up)  22.1 us
    concatenate x9, other arithmetic, with_halo(): jnp.concatenate([jnp.pad(low, around), value, jnp.pad(high, around)], axi...  10.2 us
    unnamed x50, local copies, waits for them, and re-layouts  9.1 us
    add x1, other arithmetic, local(): gradient = gradient + courant * current * forward_lap  7.69 us
    dot_general x4, matrix products, decode(): jnp.dot(masked.reshape(size_x * size_y, size_z), block_table(size_z), pre...  7.6 us
    slice x8, local copies, waits for them, and re-layouts, with_halo(): last = lax.slice_in_dim(value, length - width, length, axis=dim)  6.9 us
  transfers between devices with their start and end apart: 30, of which 11 were waited for; matrix products, arithmetic and copies ran while one was open for 13% of the time, Pallas kernels for 0%

commit v1 on v0

v1 whole, which is shorter than its diff:
```python
import functools

import jax
import jax.numpy as jnp
import numpy as np
from jax import lax
from jax.experimental import pallas as pl
from jax.experimental.pallas import tpu as pltpu
from jax.sharding import PartitionSpec as P

STAR = (-205.0 / 72.0, 8.0 / 5.0, -1.0 / 5.0, 8.0 / 315.0, -1.0 / 560.0)
CX, CY, CZ, STEPS, RECS = 16, 32, 128, 4, 128
ROWS = CX * CY
AXES = ("gx", "gy", "gz")
MESH = pl.DeviceIdType.MESH
F32, BF16 = jnp.float32, jnp.bfloat16


def split_np(table):
    high = table.astype(np.float32).astype(jnp.bfloat16)
    low = (table - high.astype(np.float64)).astype(np.float32).astype(jnp.bfloat16)
    return high, low


def tables():
    freq, place = np.arange(4)[:, None], np.arange(4)[None, :]
    dct = np.where(freq == 0, 0.5, np.sqrt(0.5)) * np.cos(np.pi * (2 * place + 1) * freq / 8)
    along_z = np.kron(np.eye(CZ // 4), dct)
    along_xy = np.kron(dct.T, np.kron(np.eye(CY // 4), dct.T))
    gap = np.abs(np.arange(CZ)[:, None] - np.arange(CZ)[None, :])
    taps = np.select([gap == k for k in range(1, 5)], STAR[1:], 0.0)
    lane = np.arange(CZ)[None, :]
    member = (np.arange(CZ) % 4)[:, None]
    below = np.select([lane + 4 - member == k for k in range(1, 5)], STAR[1:], 0.0)
    above = np.select([128 + member - lane == k for k in range(1, 5)], STAR[1:], 0.0)
    halo = np.concatenate([below, above], axis=0)
    taps_hl = np.concatenate(split_np(taps), axis=1)
    z_hl = np.concatenate(split_np(along_z), axis=1)
    halo_hl = np.concatenate(split_np(halo), axis=1)
    mats = np.stack(
        [np.concatenate([taps_hl, taps_hl]), np.concatenate([z_hl, z_hl]), halo_hl]
    )
    decode_xy = np.concatenate(split_np(along_xy), axis=1)
    spread_z = np.kron(np.eye(CZ // 4), np.ones((1, 4))).astype(jnp.bfloat16)
    spread_y = np.kron(np.eye(STEPS * CX // 4), np.kron(np.eye(CY // 4), np.ones((4, 1))))
    return mats, decode_xy, spread_z, spread_y.astype(jnp.bfloat16)


def split(value):
    high = value.astype(BF16)
    low = (value - high.astype(F32)).astype(BF16)
    return high, low


def dot(a, b):
    return lax.dot_general(a, b, (((1,), (0,)), ((), ())), preferred_element_type=F32)


def halves(value):
    return value[:, :CZ] + value[:, CZ:]


def kernel(
    coef, keep, cour, damp, nxt, now, cell, data, mats, dxy, spz, spy,
    grad_o, last_o, before_o,
    F, cin, kin, cour_v, damp_v, next_v, cell_v, data_v, mats_v, dxy_v, spz_v, spy_v,
    wa, wb, we, inj, thr, Z, E, G, last_v, XH, YP, YH, ZP, ZH,
    load_sem, store_sem, send_sem, recv_sem,
):
    me = [lax.axis_index(axis) for axis in AXES]
    size = [lax.axis_size(axis) for axis in AXES]
    has = [(me[d] > 0, me[d] < size[d] - 1) for d in range(3)]
    other = [({AXES[d]: me[d] - 1}, {AXES[d]: me[d] + 1}) for d in range(3)]

    loads = [
        pltpu.make_async_copy(src, dst, load_sem.at[n])
        for n, (src, dst) in enumerate(
            [
                (now, F.at[0, pl.ds(4, CX), pl.ds(8, CY)]),
                (mats, mats_v), (keep, kin), (spz, spz_v), (spy, spy_v), (dxy, dxy_v),
                (coef, cin), (damp, damp_v), (cour, cour_v), (nxt, next_v),
                (cell, cell_v), (data, data_v),
            ]
        )
    ]
    for load in loads:
        load.start()

    barrier = pltpu.get_barrier_semaphore()
    for d in range(3):
        for side in range(2):
            @pl.when(has[d][side])
            def _():
                pl.semaphore_signal(
                    barrier, inc=1, device_id=other[d][side], device_id_type=MESH
                )

    def clear(f, carry):
        F[f, 0:4] = jnp.zeros((4, 48, CZ), F32)
        F[f, 20:24] = jnp.zeros((4, 48, CZ), F32)
        F[f, 4:20, 0:8] = jnp.zeros((CX, 8, CZ), F32)
        F[f, 4:20, 40:48] = jnp.zeros((CX, 8, CZ), F32)
        for side in range(2):
            YH[f, side, 0:8] = jnp.zeros((8, CZ), F32)
            YH[f, side, 72:80] = jnp.zeros((8, CZ), F32)

            @pl.when(jnp.logical_not(has[0][side]))
            def _():
                XH[f, side] = jnp.zeros((4, CY, CZ), F32)

            @pl.when(jnp.logical_not(has[1][side]))
            def _():
                YH[f, side, 8:72] = jnp.zeros((64, CZ), F32)

            @pl.when(jnp.logical_not(has[2][side]))
            def _():
                ZH[f, side] = jnp.zeros((16, CZ), F32)

        return carry

    lax.fori_loop(0, 8, clear, 0)

    lane = lax.broadcasted_iota(jnp.int32, (8, CZ), 1)
    sub = lax.broadcasted_iota(jnp.int32, (8, CZ), 0)
    near_low = [None] + [jnp.where(sub < k, STAR[k], 0.0).astype(F32) for k in range(1, 5)]
    near_high = [None] + [jnp.where(sub >= 8 - k, STAR[k], 0.0).astype(F32) for k in range(1, 5)]

    def face(f, d, side):
        if d == 0:
            src = F.at[f, pl.ds(4 if side == 0 else CX, 4), pl.ds(8, CY)]
            dst = XH.at[f, 1 - side]
        elif d == 1:
            src, dst = YP.at[f, side], YH.at[f, 1 - side, pl.ds(8, 64)]
        else:
            src, dst = ZP.at[f, side], ZH.at[f, 1 - side]
        return pltpu.make_async_remote_copy(
            src_ref=src,
            dst_ref=dst,
            send_sem=send_sem.at[f, 2 * d + side],
            recv_sem=recv_sem.at[f, 2 * d + 1 - side],
            device_id=other[d][side],
            device_id_type=MESH,
        )

    def pack(f):
        def pack_y(p, carry):
            for side, row in ((0, 8), (1, 36)):
                two = [F[f, 4 + 2 * p + q, row : row + 4, :] for q in range(2)]
                YP[f, side, pl.ds(pl.multiple_of(8 * p, 8), 8), :] = jnp.concatenate(two, axis=0)
            return carry

        lax.fori_loop(0, 8, pack_y, 0, unroll=True)

        def pack_z(q, kept):
            kept = list(kept)
            for tile in range(4):
                i = 4 * q + tile
                here = lane // 4 == i
                for half in range(2):
                    value = F[f, 4 + 8 * half + q, 8 + 8 * tile : 16 + 8 * tile, :]
                    low = pltpu.roll(value, 4 * i, 1)
                    high = pltpu.roll(value, (4 * i + 4) % CZ, 1)
                    kept[half] = jnp.where(here, low, kept[half])
                    kept[2 + half] = jnp.where(here, high, kept[2 + half])
            return tuple(kept)

        zero = jnp.zeros((8, CZ), F32)
        kept = lax.fori_loop(0, 8, pack_z, (zero,) * 4, unroll=True)
        for side in range(2):
            for half in range(2):
                ZP[f, side, 8 * half : 8 * half + 8, :] = kept[2 * side + half]

    def send(f):
        for d in (1, 0, 2):
            for side in range(2):
                @pl.when(has[d][side])
                def _():
                    face(f, d, side).start()

    def arrive(f):
        for d in (0, 2, 1):
            for side in range(2):
                @pl.when(has[d][side])
                def _():
                    face(f, d, 1 - side).wait_recv()

    def own_z(f):
        value = F[f, 4:20, 8:40, :].reshape(ROWS, CZ)
        return halves(dot(jnp.concatenate(split(value), axis=1), mats_v[0]))

    def far_z(f):
        group = lax.broadcasted_iota(jnp.int32, (1, 32, 8, CZ), 1)
        lanes = lax.broadcasted_iota(jnp.int32, (1, 32, 8, CZ), 3)
        here = lanes // 4 == group
        highs, lows = [], []
        for side in range(2):
            value = ZH[f, side]
            high = value.astype(BF16).astype(F32)
            for part, out in ((high, highs), (value - high, lows)):
                wide = jnp.where(here, part.reshape(2, 1, 8, CZ), 0.0)
                out.append(wide.reshape(ROWS, CZ).astype(BF16))
        total = dot(jnp.concatenate(highs, axis=1), mats_v[2])
        total = total + dot(jnp.concatenate(lows, axis=1), mats_v[2])
        return halves(total)

    def add_far(f):
        for i in range(4):
            low = sum(STAR[k] * XH[f, 0, 4 + i - k] for k in range(i + 1, 5))
            Z[i] = Z[i] + low
            high = sum(STAR[4 + m - i] * XH[f, 1, m] for m in range(i + 1))
            Z[12 + i] = Z[12 + i] + high
        for x in range(CX):
            low = sum(near_low[k] * YH[f, 0, 12 + 4 * x - k : 20 + 4 * x - k] for k in range(1, 5))
            high = sum(near_high[k] * YH[f, 1, 4 * x + k : 4 * x + k + 8] for k in range(1, 5))
            Z[x, 0:8] = Z[x, 0:8] + low
            Z[x, 24:32] = Z[x, 24:32] + high

    def own_star(f, x):
        total = (3.0 * STAR[0]) * F[f, 4 + x, 8:40, :] + Z[x]
        for k in range(1, 5):
            pairs = F[f, 4 + x + k, 8:40, :] + F[f, 4 + x - k, 8:40, :]
            pairs = pairs + F[f, 4 + x, 8 + k : 40 + k, :] + F[f, 4 + x, 8 - k : 40 - k, :]
            total = total + STAR[k] * pairs
        return total

    def adjoint_own(s):
        Z[...] = own_z(s).reshape(CX, CY, CZ)

        def step(x, carry):
            later = next_v[x] if s == 0 else F[s - 1, 4 + x, 8:40, :]
            E[x] = (
                wa[x] * F[s, 4 + x, 8:40, :]
                - wb[x] * later
                + we[x] * own_star(s, x)
                + inj[s, x]
            )
            return carry

        lax.fori_loop(0, CX, step, 0, unroll=2)

    def adjoint_far(s):
        arrive(s)
        Z[...] = far_z(s).reshape(CX, CY, CZ)
        add_far(s)

        def step(x, carry):
            value = E[x] + we[x] * Z[x]
            if s == STEPS - 1:
                last_v[x] = value
            else:
                F[s + 1, 4 + x, 8:40, :] = value
            return carry

        lax.fori_loop(0, CX, step, 0, unroll=4)

    def decode(s):
        level = (
            lax.broadcasted_iota(jnp.int32, (CY, CZ), 0) % 4
            + lax.broadcasted_iota(jnp.int32, (CY, CZ), 1) % 4
        ).astype(F32)
        masked = [
            jnp.where(level + float(x % 4) < thr[s, x // 4], cin[s, x], 0.0) for x in range(CX)
        ]
        value = jnp.concatenate(masked, axis=0)
        along_z = halves(dot(jnp.concatenate(split(value), axis=1), mats_v[1]))
        for g in range(CX // 4):
            both = jnp.concatenate(split(along_z[CZ * g : CZ * g + CZ]), axis=1)
            out = halves(dot(dxy_v[...], jnp.concatenate([both, both], axis=0)))
            F[4 + s, 4 + 4 * g : 8 + 4 * g, 8:40, :] = out.reshape(4, CY, CZ)

    def gradient(s):
        f = 4 + s
        arrive(f)
        Z[...] = (own_z(f) + far_z(f)).reshape(CX, CY, CZ)
        add_far(f)

        def step(x, carry):
            value = cour_v[x] * F[s, 4 + x, 8:40, :] * own_star(f, x)
            G[x] = value if s == 0 else G[x] + value
            return carry

        lax.fori_loop(0, CX, step, 0, unroll=2)

    loads[0].wait()
    pack(0)
    peers = sum(there.astype(jnp.int32) for pair in has for there in pair)
    pl.semaphore_wait(barrier, peers)
    send(0)

    for load in loads[1:7]:
        load.wait()
    levels = kin[...].reshape(STEPS * (CX // 4) * (CY // 4), CZ // 4).astype(F32).astype(BF16)
    wide = dot(levels, spz_v[...]).astype(BF16)
    thr[...] = dot(spy_v[...], wide).reshape(STEPS, CX // 4, CY, CZ)
    for s in range(2):
        decode(s)
        pack(4 + s)
        send(4 + s)

    for load in loads[7:]:
        load.wait()

    def weights(x, carry):
        over = 1.0 / (1.0 + damp_v[x])
        wa[x] = 2.0 * over
        wb[x] = (1.0 - damp_v[x]) * over
        we[x] = cour_v[x] * over
        return carry

    lax.fori_loop(0, CX, weights, 0, unroll=2)

    row = lax.broadcasted_iota(jnp.int32, (ROWS, RECS), 0)
    rows_hot = jnp.where(row == cell_v[...] // CZ, 1.0, 0.0).astype(BF16)
    rows_hot = jnp.concatenate([rows_hot, rows_hot], axis=1)
    at_lane = lax.broadcasted_iota(jnp.int32, (CZ, RECS), 0) == cell_v[...] % CZ
    for s in range(STEPS):
        lanes_hot = jnp.where(at_lane, data_v[s : s + 1, :], 0.0)
        lanes_hot = jnp.concatenate(split(lanes_hot), axis=1)
        spread = lax.dot_general(
            rows_hot, lanes_hot, (((1,), (1,)), ((), ())), preferred_element_type=F32
        )
        inj[s] = spread.reshape(CX, CY, CZ) * (0.5 * wa[...])

    stores = [
        pltpu.make_async_copy(G, grad_o, store_sem.at[0]),
        pltpu.make_async_copy(last_v, last_o, store_sem.at[1]),
        pltpu.make_async_copy(
            F.at[STEPS - 1, pl.ds(4, CX), pl.ds(8, CY)], before_o, store_sem.at[2]
        ),
    ]
    adjoint_own(0)
    for s in range(STEPS):
        adjoint_far(s)
        if s < STEPS - 1:
            pack(s + 1)
            send(s + 1)
            if s == STEPS - 2:
                stores[2].start()
            if s < 2:
                decode(2 + s)
                pack(6 + s)
                send(6 + s)
            adjoint_own(s + 1)
            gradient(s)
            if s == STEPS - 2:
                gradient(s + 1)
                stores[0].start()
    stores[1].start()
    for f in range(8):
        for d in range(3):
            for side in range(2):
                @pl.when(has[d][side])
                def _():
                    face(f, d, side).wait_send()
    for store in stores:
        store.wait()


def local(coef, keep, courant, damp, adj_next, adj_now, rec_cell, rec_data):
    shape = (CX, CY, CZ)
    block = jax.ShapeDtypeStruct(shape, F32)
    mats, dxy, spz, spy = tables()
    vmem = pltpu.VMEM
    scratch = [
        vmem((8, 24, 48, CZ), F32),
        vmem((STEPS,) + shape, F32),
        vmem((STEPS, CX // 4, CY // 4, CZ // 4), jnp.int32),
        vmem(shape, F32), vmem(shape, F32), vmem(shape, F32),
        vmem((1, RECS), jnp.int32), vmem((STEPS, RECS), F32),
        vmem(mats.shape, BF16), vmem(dxy.shape, BF16), vmem(spz.shape, BF16), vmem(spy.shape, BF16),
        vmem(shape, F32), vmem(shape, F32), vmem(shape, F32),
        vmem((STEPS,) + shape, F32),
        vmem((STEPS, CX // 4, CY, CZ), F32),
        vmem(shape, F32), vmem(shape, F32), vmem(shape, F32), vmem(shape, F32),
        vmem((8, 2, 4, CY, CZ), F32),
        vmem((8, 2, 64, CZ), F32), vmem((8, 2, 80, CZ), F32),
        vmem((8, 2, 16, CZ), F32), vmem((8, 2, 16, CZ), F32),
        pltpu.SemaphoreType.DMA((12,)), pltpu.SemaphoreType.DMA((3,)),
        pltpu.SemaphoreType.DMA((8, 6)), pltpu.SemaphoreType.DMA((8, 6)),
    ]
    anywhere = pl.BlockSpec(memory_space=pl.ANY)
    return pl.pallas_call(
        kernel,
        out_shape=(block, block, block),
        in_specs=[pl.BlockSpec(memory_space=pltpu.HBM)] * 12,
        out_specs=(anywhere,) * 3,
        scratch_shapes=scratch,
        compiler_params=pltpu.CompilerParams(
            collective_id=0, has_side_effects=True, vmem_limit_bytes=48 * 1024 * 1024
        ),
        name="adjoint_window",
    )(
        coef, keep, courant, damp, adj_next, adj_now,
        rec_cell.reshape(1, RECS), rec_data.reshape(STEPS, RECS),
        jnp.asarray(mats), jnp.asarray(dxy), jnp.asarray(spz), jnp.asarray(spy),
    )


def solution(mesh):
    field = P("gx", "gy", "gz")
    in_specs = (
        P(None, "gx", "gy", "gz"), P(None, "gx", "gy", "gz"),
        field, field, field, field,
        P("gx", "gy", "gz", None), P("gx", "gy", "gz", None, None),
    )
    return jax.shard_map(
        local, mesh=mesh, in_specs=in_specs, out_specs=(field,) * 3, check_vma=False
    )
```

time: 199 us -> 42.6 us (0.21)
  the two profiles are of different devices: /device:TPU:62 before, /device:TPU:24 now
where the time goes in v1:
time: 42.6 us; the launch traced here: 42.1 us
  Pallas kernels  29.4 us (69%)
  local copies, waits for them, and re-layouts  12.1 us (28%)
  between operations  0.67 us (2%)
    pallas_call x1, Pallas kernels, local(): pl.pallas_call(kernel, out_shape=(block, block, block), in_specs=[pl.Bloc...  29.4 us
    unnamed x27, local copies, waits for them, and re-layouts  12.1 us

profile of v1, /device:TPU:24, one launch (start us, length us, event | category | flops | bytes accessed | tf_op | source)
XLA Modules:
  0.0 42.1 jit_solution(4459573477353298939)
XLA Ops:
  0.6 0.0 copy-start.10
  0.6 0.0 copy-start.11
  0.7 0.7 %copy-done.10 = f32[1,1,1,4,128]{4,3,2,1,0:T(4,128)S(1)} copy-done((f32[1,1,1,4,128]{4,3,2,1,0:T(4,128)S(1)}, f32[1,1,1,4,128]{4,3,2,1,0:T(4,128)}, u32[]{:S(2)}) %copy-start.10) | copy-done | bytes 2072
  1.3 0.0 copy-done.11
  1.3 0.0 copy-start
  1.3 1.2 %copy-done = f32[4,16,32,128]{3,2,1,0:T(8,128)S(1)} copy-done((f32[4,16,32,128]{3,2,1,0:T(8,128)S(1)}, f32[4,16,32,128]{3,2,1,0:T(8,128)}, u32[]{:S(2)}) %copy-start) | copy-done | bytes 1048600
  2.5 0.0 copy-start.1
  2.5 1.0 %copy-done.1 = bf16[3,256,256]{2,1,0:T(8,128)(2,1)S(1)} copy-done((bf16[3,256,256]{2,1,0:T(8,128)(2,1)S(1)}, bf16[3,256,256]{2,1,0:T(8,128)(2,1)}, u32[]{:S(2)}) %copy-start.1) | copy-done | bytes 393240
  3.5 0.0 copy-start.2
  3.5 0.9 %copy-done.2 = f32[16,32,128]{2,1,0:T(8,128)S(1)} copy-done((f32[16,32,128]{2,1,0:T(8,128)S(1)}, f32[16,32,128]{2,1,0:T(8,128)}, u32[]{:S(2)}) %copy-start.2) | copy-done | bytes 262168
  4.5 0.0 copy-start.3
  4.5 0.9 %copy-done.3 = f32[16,32,128]{2,1,0:T(8,128)S(1)} copy-done((f32[16,32,128]{2,1,0:T(8,128)S(1)}, f32[16,32,128]{2,1,0:T(8,128)}, u32[]{:S(2)}) %copy-start.3) | copy-done | bytes 262168
  5.4 0.0 copy-start.4
  5.4 0.9 %copy-done.4 = f32[16,32,128]{2,1,0:T(8,128)S(1)} copy-done((f32[16,32,128]{2,1,0:T(8,128)S(1)}, f32[16,32,128]{2,1,0:T(8,128)}, u32[]{:S(2)}) %copy-start.4) | copy-done | bytes 262168
  6.4 0.0 copy-start.5
  6.4 0.9 %copy-done.5 = f32[16,32,128]{2,1,0:T(8,128)S(1)} copy-done((f32[16,32,128]{2,1,0:T(8,128)S(1)}, f32[16,32,128]{2,1,0:T(8,128)}, u32[]{:S(2)}) %copy-start.5) | copy-done | bytes 262168
  7.3 0.0 copy-start.6
  7.3 0.9 %copy-done.6 = bf16[512,128]{1,0:T(8,128)(2,1)S(1)} copy-done((bf16[512,128]{1,0:T(8,128)(2,1)S(1)}, bf16[512,128]{1,0:T(8,128)(2,1)}, u32[]{:S(2)}) %copy-start.6) | copy-done | bytes 131096
  8.2 0.0 copy-start.7
  8.2 0.8 %copy-done.7 = s32[4,4,8,32]{3,2,1,0:T(8,128)S(1)} copy-done((s32[4,4,8,32]{3,2,1,0:T(8,128)S(1)}, s32[4,4,8,32]{3,2,1,0:T(8,128)}, u32[]{:S(2)}) %copy-start.7) | copy-done | bytes 16408
  9.1 0.0 copy-start.8
  9.1 0.8 %copy-done.8 = bf16[128,256]{1,0:T(8,128)(2,1)S(1)} copy-done((bf16[128,256]{1,0:T(8,128)(2,1)S(1)}, bf16[128,256]{1,0:T(8,128)(2,1)}, u32[]{:S(2)}) %copy-start.8) | copy-done | bytes 65560
  9.9 0.0 copy-start.9
  9.9 0.7 %copy-done.9 = bf16[32,128]{1,0:T(8,128)(2,1)S(1)} copy-done((bf16[32,128]{1,0:T(8,128)(2,1)S(1)}, bf16[32,128]{1,0:T(8,128)(2,1)}, u32[]{:S(2)}) %copy-start.9) | copy-done | bytes 8216
  10.6 29.4 %adjoint_window.1 = (f32[16,32,128]{2,1,0:T(8,128)S(1)}, f32[16,32,128]{2,1,0:T(8,128)S(1)}, f32[16,32,128]{2,1,0:T(8,128)S(1)}) custom-call(f32[4,16,32,128]{3,2,1,0:T(8,128)S(1)} %copy-done, s32[4,4,8,32]{3,2,1,0:T(8,128)S(1)} %copy-done.7, f32[16,32,128]{2,1,0:T(8,128)S(1)} %copy-done.2, f32[16,32,128]{2,1,0:T(8,128)S(1)} %copy-done.3, ...), custom_call_target="tpu_custom_call" | custom-call | tf_op jit(solution)/shard_map/adjoint_window/pallas_call | solution.py:382
  40.0 0.7 %copy.18 = f32[16,32,128]{2,1,0:T(8,128)} copy(f32[16,32,128]{2,1,0:T(8,128)S(1)} %get-tuple-element.6) | data formatting | bytes 524288
  40.7 0.7 %copy.19 = f32[16,32,128]{2,1,0:T(8,128)} copy(f32[16,32,128]{2,1,0:T(8,128)S(1)} %get-tuple-element.7) | data formatting | bytes 524288
  41.4 0.7 %copy.20 = f32[16,32,128]{2,1,0:T(8,128)} copy(f32[16,32,128]{2,1,0:T(8,128)S(1)} %get-tuple-element.8) | data formatting | bytes 524288
Async XLA Ops:
  0.6 0.7 %copy-start.10 = (f32[1,1,1,4,128]{4,3,2,1,0:T(4,128)S(1)}, f32[1,1,1,4,128]{4,3,2,1,0:T(4,128)}, u32[]{:S(2)}) copy-start(f32[1,1,1,4,128]{4,3,2,1,0:T(4,128)} %param.19) | copy-start | bytes 6148
  0.6 0.7 %copy-start.11 = (s32[1,1,1,128]{3,2,1,0:T(1,128)S(1)}, s32[1,1,1,128]{3,2,1,0:T(1,128)}, u32[]{:S(2)}) copy-start(s32[1,1,1,128]{3,2,1,0:T(1,128)} %param.18) | copy-start | bytes 1540
  1.3 1.2 %copy-start = (f32[4,16,32,128]{3,2,1,0:T(8,128)S(1)}, f32[4,16,32,128]{3,2,1,0:T(8,128)}, u32[]{:S(2)}) copy-start(f32[4,16,32,128]{3,2,1,0:T(8,128)} %coef.1) | copy-start | bytes 3145732
  2.5 1.0 %copy-start.1 = (bf16[3,256,256]{2,1,0:T(8,128)(2,1)S(1)}, bf16[3,256,256]{2,1,0:T(8,128)(2,1)}, u32[]{:S(2)}) copy-start(bf16[3,256,256]{2,1,0:T(8,128)(2,1)} %constant.8.clone.mats) | copy-start | bytes 1179652
  3.5 0.9 %copy-start.2 = (f32[16,32,128]{2,1,0:T(8,128)S(1)}, f32[16,32,128]{2,1,0:T(8,128)}, u32[]{:S(2)}) copy-start(f32[16,32,128]{2,1,0:T(8,128)} %cour.1) | copy-start | bytes 786436
  4.5 0.9 %copy-start.3 = (f32[16,32,128]{2,1,0:T(8,128)S(1)}, f32[16,32,128]{2,1,0:T(8,128)}, u32[]{:S(2)}) copy-start(f32[16,32,128]{2,1,0:T(8,128)} %damp.1) | copy-start | bytes 786436
  5.4 0.9 %copy-start.4 = (f32[16,32,128]{2,1,0:T(8,128)S(1)}, f32[16,32,128]{2,1,0:T(8,128)}, u32[]{:S(2)}) copy-start(f32[16,32,128]{2,1,0:T(8,128)} %nxt.1) | copy-start | bytes 786436
  6.4 0.9 %copy-start.5 = (f32[16,32,128]{2,1,0:T(8,128)S(1)}, f32[16,32,128]{2,1,0:T(8,128)}, u32[]{:S(2)}) copy-start(f32[16,32,128]{2,1,0:T(8,128)} %now.1) | copy-start | bytes 786436
  7.3 0.9 %copy-start.6 = (bf16[512,128]{1,0:T(8,128)(2,1)S(1)}, bf16[512,128]{1,0:T(8,128)(2,1)}, u32[]{:S(2)}) copy-start(bf16[512,128]{1,0:T(8,128)(2,1)} %constant.11.clone.spy) | copy-start | bytes 393220
  8.2 0.8 %copy-start.7 = (s32[4,4,8,32]{3,2,1,0:T(8,128)S(1)}, s32[4,4,8,32]{3,2,1,0:T(8,128)}, u32[]{:S(2)}) copy-start(s32[4,4,8,32]{3,2,1,0:T(8,128)} %keep.1) | copy-start | bytes 49156
  9.1 0.8 %copy-start.8 = (bf16[128,256]{1,0:T(8,128)(2,1)S(1)}, bf16[128,256]{1,0:T(8,128)(2,1)}, u32[]{:S(2)}) copy-start(bf16[128,256]{1,0:T(8,128)(2,1)} %constant.9.clone.dxy) | copy-start | bytes 196612
  9.9 0.7 %copy-start.9 = (bf16[32,128]{1,0:T(8,128)(2,1)S(1)}, bf16[32,128]{1,0:T(8,128)(2,1)}, u32[]{:S(2)}) copy-start(bf16[32,128]{1,0:T(8,128)(2,1)} %constant.10.clone.spz) | copy-start | bytes 24580

commit v2 on v1

--- a/solution.py
+++ b/solution.py
@@ -64,8 +64,8 @@
     coef, keep, cour, damp, nxt, now, cell, data, mats, dxy, spz, spy,
     grad_o, last_o, before_o,
     F, cin, kin, cour_v, damp_v, next_v, cell_v, data_v, mats_v, dxy_v, spz_v, spy_v,
-    wa, wb, we, inj, thr, Z, E, G, last_v, XH, YP, YH, ZP, ZH,
-    load_sem, store_sem, send_sem, recv_sem,
+    wa, wb, we, inj, thr, Z, E, XH, YP, YH, ZP, ZH,
+    load_sem, send_sem, recv_sem,
 ):
     me = [lax.axis_index(axis) for axis in AXES]
     size = [lax.axis_size(axis) for axis in AXES]
@@ -246,9 +246,11 @@
         def step(x, carry):
             value = E[x] + we[x] * Z[x]
             if s == STEPS - 1:
-                last_v[x] = value
+                last_o[x] = value
             else:
                 F[s + 1, 4 + x, 8:40, :] = value
+            if s == STEPS - 2:
+                before_o[x] = value
             return carry
 
         lax.fori_loop(0, CX, step, 0, unroll=4)
@@ -276,7 +278,7 @@
 
         def step(x, carry):
             value = cour_v[x] * F[s, 4 + x, 8:40, :] * own_star(f, x)
-            G[x] = value if s == 0 else G[x] + value
+            grad_o[x] = value if s == 0 else grad_o[x] + value
             return carry
 
         lax.fori_loop(0, CX, step, 0, unroll=2)
@@ -321,21 +323,12 @@
         )
         inj[s] = spread.reshape(CX, CY, CZ) * (0.5 * wa[...])
 
-    stores = [
-        pltpu.make_async_copy(G, grad_o, store_sem.at[0]),
-        pltpu.make_async_copy(last_v, last_o, store_sem.at[1]),
-        pltpu.make_async_copy(
-            F.at[STEPS - 1, pl.ds(4, CX), pl.ds(8, CY)], before_o, store_sem.at[2]
-        ),
-    ]
     adjoint_own(0)
     for s in range(STEPS):
         adjoint_far(s)
         if s < STEPS - 1:
             pack(s + 1)
             send(s + 1)
-            if s == STEPS - 2:
-                stores[2].start()
             if s < 2:
                 decode(2 + s)
                 pack(6 + s)
@@ -344,16 +337,21 @@
             gradient(s)
             if s == STEPS - 2:
                 gradient(s + 1)
-                stores[0].start()
-    stores[1].start()
     for f in range(8):
         for d in range(3):
             for side in range(2):
                 @pl.when(has[d][side])
                 def _():
                     face(f, d, side).wait_send()
-    for store in stores:
-        store.wait()
+
+
+def put_out(grad_v, last_v, before_v, grad_o, last_o, before_o, sem):
+    pairs = ((grad_v, grad_o), (last_v, last_o), (before_v, before_o))
+    copies = [pltpu.make_async_copy(v, o, sem.at[n]) for n, (v, o) in enumerate(pairs)]
+    for copy in copies:
+        copy.start()
+    for copy in copies:
+        copy.wait()
 
 
 def local(coef, keep, courant, damp, adj_next, adj_now, rec_cell, rec_data):
@@ -371,22 +369,23 @@
         vmem(shape, F32), vmem(shape, F32), vmem(shape, F32),
         vmem((STEPS,) + shape, F32),
         vmem((STEPS, CX // 4, CY, CZ), F32),
-        vmem(shape, F32), vmem(shape, F32), vmem(shape, F32), vmem(shape, F32),
+        vmem(shape, F32), vmem(shape, F32),
         vmem((8, 2, 4, CY, CZ), F32),
         vmem((8, 2, 64, CZ), F32), vmem((8, 2, 80, CZ), F32),
         vmem((8, 2, 16, CZ), F32), vmem((8, 2, 16, CZ), F32),
-        pltpu.SemaphoreType.DMA((12,)), pltpu.SemaphoreType.DMA((3,)),
+        pltpu.SemaphoreType.DMA((12,)),
         pltpu.SemaphoreType.DMA((8, 6)), pltpu.SemaphoreType.DMA((8, 6)),
     ]
-    anywhere = pl.BlockSpec(memory_space=pl.ANY)
-    return pl.pallas_call(
+    vmem_spec = pl.BlockSpec(memory_space=pltpu.VMEM)
+    hbm_spec = pl.BlockSpec(memory_space=pltpu.HBM)
+    results = pl.pallas_call(
         kernel,
-        out_shape=(block, block, block),
-        in_specs=[pl.BlockSpec(memory_space=pltpu.HBM)] * 12,
-        out_specs=(anywhere,) * 3,
+        out_shape=(vmem(shape, F32),) * 3,
+        in_specs=[hbm_spec] * 12,
+        out_specs=(vmem_spec,) * 3,
         scratch_shapes=scratch,
         compiler_params=pltpu.CompilerParams(
-            collective_id=0, has_side_effects=True, vmem_limit_bytes=48 * 1024 * 1024
+            collective_id=0, has_side_effects=True, vmem_limit_bytes=67043328 - 3 * 4 * CX * CY * CZ
         ),
         name="adjoint_window",
     )(
@@ -394,6 +393,15 @@
         rec_cell.reshape(1, RECS), rec_data.reshape(STEPS, RECS),
         jnp.asarray(mats), jnp.asarray(dxy), jnp.asarray(spz), jnp.asarray(spy),
     )
+    return pl.pallas_call(
+        put_out,
+        out_shape=(block,) * 3,
+        in_specs=[pl.BlockSpec(memory_space=pl.ANY)] * 3,
+        out_specs=(hbm_spec,) * 3,
+        scratch_shapes=[pltpu.SemaphoreType.DMA((3,))],
+        compiler_params=pltpu.CompilerParams(vmem_limit_bytes=1024 * 1024),
+        name="put_out",
+    )(*results)
 
 
 def solution(mesh):

time: 42.6 us -> 30.9 us (0.73)
  local copies, waits for them, and re-layouts: 12.1 us -> 0 us
  Pallas kernels: 29.4 us -> 30 us
    unnamed x27 -> x0, local copies, waits for them, and re-layouts: 12.1 us -> none
    pallas_call x1 -> x2, Pallas kernels: 29.4 us -> 30 us  [the longest x1 29.1 us: local(): pl.pallas_call(kernel, out_shape=(vmem(shape, F32),) * 3, in_specs=[hbm_s...]
where the time goes in v2:
time: 30.9 us; the launch traced here: 30.6 us
  Pallas kernels  30 us (97%)
  between operations  0.64 us (2%)
    pallas_call x1, Pallas kernels, local(): pl.pallas_call(kernel, out_shape=(vmem(shape, F32),) * 3, in_specs=[hbm_s...  29.1 us
    pallas_call x1, Pallas kernels, local(): pl.pallas_call(put_out, out_shape=(block,) * 3, in_specs=[pl.BlockSpec(me...  0.9 us

profile of v2, /device:TPU:24, one launch (start us, length us, event | category | flops | bytes accessed | tf_op | source)
XLA Modules:
  0.0 30.6 jit_solution(18380332412514933844)
XLA Ops:
  0.6 29.1 %adjoint_window.1 = (f32[16,32,128]{2,1,0:T(8,128)S(1)}, f32[16,32,128]{2,1,0:T(8,128)S(1)}, f32[16,32,128]{2,1,0:T(8,128)S(1)}) custom-call(f32[4,16,32,128]{3,2,1,0:T(8,128)} %coef.1, s32[4,4,8,32]{3,2,1,0:T(8,128)} %keep.1, f32[16,32,128]{2,1,0:T(8,128)} %cour.1, f32[16,32,128]{2,1,0:T(8,128)} %damp.1, f32[16,32,128]{2,1,0:T(8,128)} %nxt.1, ...), custom_call_target="tpu_custom_call" | custom-call | tf_op jit(solution)/shard_map/adjoint_window/pallas_call | solution.py:381
  29.7 0.9 %put_out.1 = (f32[16,32,128]{2,1,0:T(8,128)}, f32[16,32,128]{2,1,0:T(8,128)}, f32[16,32,128]{2,1,0:T(8,128)}) custom-call(f32[16,32,128]{2,1,0:T(8,128)S(1)} %get-tuple-element.6.grad_v, f32[16,32,128]{2,1,0:T(8,128)S(1)} %get-tuple-element.7.last_v, f32[16,32,128]{2,1,0:T(8,128)S(1)} %get-tuple-element.8.before_v), custom_call_target="tpu_custom_call" | custom-call | tf_op jit(solution)/shard_map/put_out/pallas_call | solution.py:396

commit v3 on v2

--- a/solution.py
+++ b/solution.py
@@ -11,6 +11,8 @@
 STAR = (-205.0 / 72.0, 8.0 / 5.0, -1.0 / 5.0, 8.0 / 315.0, -1.0 / 560.0)
 CX, CY, CZ, STEPS, RECS = 16, 32, 128, 4, 128
 ROWS = CX * CY
+PIECES = 2
+PART = 64 // PIECES
 AXES = ("gx", "gy", "gz")
 MESH = pl.DeviceIdType.MESH
 F32, BF16 = jnp.float32, jnp.bfloat16
@@ -29,16 +31,10 @@
     along_xy = np.kron(dct.T, np.kron(np.eye(CY // 4), dct.T))
     gap = np.abs(np.arange(CZ)[:, None] - np.arange(CZ)[None, :])
     taps = np.select([gap == k for k in range(1, 5)], STAR[1:], 0.0)
-    lane = np.arange(CZ)[None, :]
-    member = (np.arange(CZ) % 4)[:, None]
-    below = np.select([lane + 4 - member == k for k in range(1, 5)], STAR[1:], 0.0)
-    above = np.select([128 + member - lane == k for k in range(1, 5)], STAR[1:], 0.0)
-    halo = np.concatenate([below, above], axis=0)
     taps_hl = np.concatenate(split_np(taps), axis=1)
     z_hl = np.concatenate(split_np(along_z), axis=1)
-    halo_hl = np.concatenate(split_np(halo), axis=1)
     mats = np.stack(
-        [np.concatenate([taps_hl, taps_hl]), np.concatenate([z_hl, z_hl]), halo_hl]
+        [np.concatenate([taps_hl, taps_hl]), np.concatenate([z_hl, z_hl])]
     )
     decode_xy = np.concatenate(split_np(along_xy), axis=1)
     spread_z = np.kron(np.eye(CZ // 4), np.ones((1, 4))).astype(jnp.bfloat16)
@@ -64,7 +60,7 @@
     coef, keep, cour, damp, nxt, now, cell, data, mats, dxy, spz, spy,
     grad_o, last_o, before_o,
     F, cin, kin, cour_v, damp_v, next_v, cell_v, data_v, mats_v, dxy_v, spz_v, spy_v,
-    wa, wb, we, inj, thr, Z, E, XH, YP, YH, ZP, ZH,
+    wa, wb, we, inj, thr, Z, XH, YP, YH, ZP, ZH,
     load_sem, send_sem, recv_sem,
 ):
     me = [lax.axis_index(axis) for axis in AXES]
@@ -101,8 +97,9 @@
         F[f, 4:20, 0:8] = jnp.zeros((CX, 8, CZ), F32)
         F[f, 4:20, 40:48] = jnp.zeros((CX, 8, CZ), F32)
         for side in range(2):
-            YH[f, side, 0:8] = jnp.zeros((8, CZ), F32)
-            YH[f, side, 72:80] = jnp.zeros((8, CZ), F32)
+            for n in range(PIECES):
+                YH[f, side, n, 0:8] = jnp.zeros((8, CZ), F32)
+                YH[f, side, n, 8 + PART : 16 + PART] = jnp.zeros((8, CZ), F32)
 
             @pl.when(jnp.logical_not(has[0][side]))
             def _():
@@ -110,7 +107,7 @@
 
             @pl.when(jnp.logical_not(has[1][side]))
             def _():
-                YH[f, side, 8:72] = jnp.zeros((64, CZ), F32)
+                YH[f, side, :, 8 : 8 + PART] = jnp.zeros((PIECES, PART, CZ), F32)
 
             @pl.when(jnp.logical_not(has[2][side]))
             def _():
@@ -125,24 +122,52 @@
     near_low = [None] + [jnp.where(sub < k, STAR[k], 0.0).astype(F32) for k in range(1, 5)]
     near_high = [None] + [jnp.where(sub >= 8 - k, STAR[k], 0.0).astype(F32) for k in range(1, 5)]
 
-    def face(f, d, side):
+    def faces(f, d, side, some=slice(None)):
         if d == 0:
-            src = F.at[f, pl.ds(4 if side == 0 else CX, 4), pl.ds(8, CY)]
-            dst = XH.at[f, 1 - side]
+            start = 4 if side == 0 else CX
+            rows = ((8, 16), (0, 8), (24, 8)) if f < STEPS else ((0, CY),)
+            pairs = [
+                (
+                    F.at[f, pl.ds(start, 4), pl.ds(8 + row, count)],
+                    XH.at[f, 1 - side, slice(None), pl.ds(row, count)],
+                )
+                for row, count in rows
+            ]
         elif d == 1:
-            src, dst = YP.at[f, side], YH.at[f, 1 - side, pl.ds(8, 64)]
+            pairs = [
+                (YP.at[f, side, pl.ds(PART * n, PART)], YH.at[f, 1 - side, n, pl.ds(8, PART)])
+                for n in range(PIECES)
+            ]
         else:
-            src, dst = ZP.at[f, side], ZH.at[f, 1 - side]
-        return pltpu.make_async_remote_copy(
-            src_ref=src,
-            dst_ref=dst,
-            send_sem=send_sem.at[f, 2 * d + side],
-            recv_sem=recv_sem.at[f, 2 * d + 1 - side],
-            device_id=other[d][side],
-            device_id_type=MESH,
-        )
-
-    def pack(f):
+            pairs = [(ZP.at[f, side], ZH.at[f, 1 - side])]
+        return [
+            pltpu.make_async_remote_copy(
+                src_ref=src,
+                dst_ref=dst,
+                send_sem=send_sem.at[f, 2 * d + side, n],
+                recv_sem=recv_sem.at[f, 2 * d + 1 - side, n],
+                device_id=other[d][side],
+                device_id_type=MESH,
+            )
+            for n, (src, dst) in list(enumerate(pairs))[some]
+        ]
+
+    def each_side(d, act):
+        for side in range(2):
+            @pl.when(has[d][side])
+            def _():
+                act(side)
+
+    def send(f, d, some=slice(None)):
+        each_side(d, lambda side: [copy.start() for copy in faces(f, d, side, some)])
+
+    def arrive(f, d, some=slice(None)):
+        each_side(d, lambda side: [copy.wait_recv() for copy in faces(f, d, 1 - side, some)])
+
+    def drain(f, d):
+        each_side(d, lambda side: [copy.wait_send() for copy in faces(f, d, side)])
+
+    def pack_rows(f):
         def pack_y(p, carry):
             for side, row in ((0, 8), (1, 36)):
                 two = [F[f, 4 + 2 * p + q, row : row + 4, :] for q in range(2)]
@@ -151,6 +176,7 @@
 
         lax.fori_loop(0, 8, pack_y, 0, unroll=True)
 
+    def pack_lanes(f):
         def pack_z(q, kept):
             kept = list(kept)
             for tile in range(4):
@@ -170,50 +196,55 @@
             for half in range(2):
                 ZP[f, side, 8 * half : 8 * half + 8, :] = kept[2 * side + half]
 
-    def send(f):
-        for d in (1, 0, 2):
-            for side in range(2):
-                @pl.when(has[d][side])
-                def _():
-                    face(f, d, side).start()
-
-    def arrive(f):
-        for d in (0, 2, 1):
-            for side in range(2):
-                @pl.when(has[d][side])
-                def _():
-                    face(f, d, 1 - side).wait_recv()
-
     def own_z(f):
         value = F[f, 4:20, 8:40, :].reshape(ROWS, CZ)
         return halves(dot(jnp.concatenate(split(value), axis=1), mats_v[0]))
 
     def far_z(f):
-        group = lax.broadcasted_iota(jnp.int32, (1, 32, 8, CZ), 1)
-        lanes = lax.broadcasted_iota(jnp.int32, (1, 32, 8, CZ), 3)
-        here = lanes // 4 == group
-        highs, lows = [], []
-        for side in range(2):
-            value = ZH[f, side]
-            high = value.astype(BF16).astype(F32)
-            for part, out in ((high, highs), (value - high, lows)):
-                wide = jnp.where(here, part.reshape(2, 1, 8, CZ), 0.0)
-                out.append(wide.reshape(ROWS, CZ).astype(BF16))
-        total = dot(jnp.concatenate(highs, axis=1), mats_v[2])
-        total = total + dot(jnp.concatenate(lows, axis=1), mats_v[2])
-        return halves(total)
-
-    def add_far(f):
+        member = lane % 4
+        out = []
+        for half in range(2):
+            low = ZH[f, 0, 8 * half : 8 * half + 8, :]
+            high = ZH[f, 1, 8 * half : 8 * half + 8, :]
+            low_sum = STAR[4] * low
+            high_sum = STAR[4] * high
+            for k in range(1, 4):
+                gap = 4 - k
+                low_sum = low_sum + jnp.where(
+                    member < k, STAR[k] * pltpu.roll(low, CZ - gap, 1), 0.0
+                )
+                high_sum = high_sum + jnp.where(
+                    member >= gap, STAR[k] * pltpu.roll(high, gap, 1), 0.0
+                )
+            out.append((low_sum, high_sum))
+        return out
+
+    def add_z(f, target, scale):
+        packed = far_z(f)
+        for v in range(64):
+            half, i = divmod(v, 32)
+            low = pltpu.roll(packed[half][0], (CZ - 4 * i) % CZ, 1)
+            high = pltpu.roll(packed[half][1], (252 - 4 * i) % CZ, 1)
+            value = jnp.where(lane < 4, low, jnp.where(lane >= CZ - 4, high, 0.0))
+            x, row = v // 4, 8 * (v % 4)
+            if scale is not None:
+                value = scale[x, row : row + 8] * value
+            target[x, row : row + 8] = target[x, row : row + 8] + value
+
+    def add_x(f, target, scale):
         for i in range(4):
             low = sum(STAR[k] * XH[f, 0, 4 + i - k] for k in range(i + 1, 5))
-            Z[i] = Z[i] + low
             high = sum(STAR[4 + m - i] * XH[f, 1, m] for m in range(i + 1))
-            Z[12 + i] = Z[12 + i] + high
-        for x in range(CX):
-            low = sum(near_low[k] * YH[f, 0, 12 + 4 * x - k : 20 + 4 * x - k] for k in range(1, 5))
-            high = sum(near_high[k] * YH[f, 1, 4 * x + k : 4 * x + k + 8] for k in range(1, 5))
-            Z[x, 0:8] = Z[x, 0:8] + low
-            Z[x, 24:32] = Z[x, 24:32] + high
+            if scale is not None:
+                low, high = scale[i] * low, scale[12 + i] * high
+            target[i] = target[i] + low
+            target[12 + i] = target[12 + i] + high
+
+    def near_y(f, x):
+        n, at = divmod(4 * x, PART)
+        low = sum(near_low[k] * YH[f, 0, n, 12 + at - k : 20 + at - k] for k in range(1, 5))
+        high = sum(near_high[k] * YH[f, 1, n, at + k : at + k + 8] for k in range(1, 5))
+        return low, high
 
     def own_star(f, x):
         total = (3.0 * STAR[0]) * F[f, 4 + x, 8:40, :] + Z[x]
@@ -223,37 +254,53 @@
             total = total + STAR[k] * pairs
         return total
 
+    def target_of(s):
+        return last_o if s == STEPS - 1 else F.at[s + 1, pl.ds(4, CX), pl.ds(8, CY)]
+
     def adjoint_own(s):
         Z[...] = own_z(s).reshape(CX, CY, CZ)
+        target = target_of(s)
 
         def step(x, carry):
             later = next_v[x] if s == 0 else F[s - 1, 4 + x, 8:40, :]
-            E[x] = (
-                wa[x] * F[s, 4 + x, 8:40, :]
-                - wb[x] * later
-                + we[x] * own_star(s, x)
-                + inj[s, x]
-            )
+            current = F[s, 4 + x, 8:40, :]
+            target[x] = wa[x] * current - wb[x] * later + we[x] * own_star(s, x) + inj[s, x]
+            if s == STEPS - 1:
+                before_o[x] = current
             return carry
 
         lax.fori_loop(0, CX, step, 0, unroll=2)
 
     def adjoint_far(s):
-        arrive(s)
-        Z[...] = far_z(s).reshape(CX, CY, CZ)
-        add_far(s)
-
-        def step(x, carry):
-            value = E[x] + we[x] * Z[x]
-            if s == STEPS - 1:
-                last_o[x] = value
-            else:
-                F[s + 1, 4 + x, 8:40, :] = value
-            if s == STEPS - 2:
-                before_o[x] = value
-            return carry
-
-        lax.fori_loop(0, CX, step, 0, unroll=4)
+        target = target_of(s)
+        sends = s < STEPS - 1
+        arrive(s, 2)
+        add_z(s, target, we)
+        arrive(s, 0)
+        add_x(s, target, we)
+        if sends:
+            send(s + 1, 0, slice(0, 1))
+        for piece in range(PIECES):
+            arrive(s, 1, slice(piece, piece + 1))
+            for p in range(8 * piece // PIECES, 8 * (piece + 1) // PIECES):
+                lows, highs = [], []
+                for x in (2 * p, 2 * p + 1):
+                    low, high = near_y(s, x)
+                    low = target[x, 0:8] + we[x, 0:8] * low
+                    high = target[x, 24:32] + we[x, 24:32] * high
+                    lows.append(low[0:4])
+                    highs.append(high[4:8])
+                    target[x, 0:8] = low
+                    target[x, 24:32] = high
+                if sends:
+                    YP[s + 1, 0, 8 * p : 8 * p + 8] = jnp.concatenate(lows, axis=0)
+                    YP[s + 1, 1, 8 * p : 8 * p + 8] = jnp.concatenate(highs, axis=0)
+            if sends:
+                send(s + 1, 1, slice(piece, piece + 1))
+        if sends:
+            send(s + 1, 0, slice(1, 3))
+            pack_lanes(s + 1)
+            send(s + 1, 2)
 
     def decode(s):
         level = (
@@ -272,9 +319,16 @@
 
     def gradient(s):
         f = 4 + s
-        arrive(f)
-        Z[...] = (own_z(f) + far_z(f)).reshape(CX, CY, CZ)
-        add_far(f)
+        Z[...] = own_z(f).reshape(CX, CY, CZ)
+        arrive(f, 2)
+        add_z(f, Z, None)
+        arrive(f, 0)
+        add_x(f, Z, None)
+        arrive(f, 1)
+        for x in range(CX):
+            low, high = near_y(f, x)
+            Z[x, 0:8] = Z[x, 0:8] + low
+            Z[x, 24:32] = Z[x, 24:32] + high
 
         def step(x, carry):
             value = cour_v[x] * F[s, 4 + x, 8:40, :] * own_star(f, x)
@@ -283,11 +337,20 @@
 
         lax.fori_loop(0, CX, step, 0, unroll=2)
 
+    def send_forward(s):
+        decode(s)
+        pack_rows(4 + s)
+        pack_lanes(4 + s)
+        for d in (1, 0, 2):
+            send(4 + s, d)
+
     loads[0].wait()
-    pack(0)
+    pack_rows(0)
+    pack_lanes(0)
     peers = sum(there.astype(jnp.int32) for pair in has for there in pair)
     pl.semaphore_wait(barrier, peers)
-    send(0)
+    for d in (1, 0, 2):
+        send(0, d)
 
     for load in loads[1:7]:
         load.wait()
@@ -295,9 +358,7 @@
     wide = dot(levels, spz_v[...]).astype(BF16)
     thr[...] = dot(spy_v[...], wide).reshape(STEPS, CX // 4, CY, CZ)
     for s in range(2):
-        decode(s)
-        pack(4 + s)
-        send(4 + s)
+        send_forward(s)
 
     for load in loads[7:]:
         load.wait()
@@ -327,22 +388,15 @@
     for s in range(STEPS):
         adjoint_far(s)
         if s < STEPS - 1:
-            pack(s + 1)
-            send(s + 1)
             if s < 2:
-                decode(2 + s)
-                pack(6 + s)
-                send(6 + s)
+                send_forward(2 + s)
             adjoint_own(s + 1)
             gradient(s)
             if s == STEPS - 2:
                 gradient(s + 1)
-    for f in range(8):
+    for f in range(2 * STEPS):
         for d in range(3):
-            for side in range(2):
-                @pl.when(has[d][side])
-                def _():
-                    face(f, d, side).wait_send()
+            drain(f, d)
 
 
 def put_out(grad_v, last_v, before_v, grad_o, last_o, before_o, sem):
@@ -369,12 +423,12 @@
         vmem(shape, F32), vmem(shape, F32), vmem(shape, F32),
         vmem((STEPS,) + shape, F32),
         vmem((STEPS, CX // 4, CY, CZ), F32),
-        vmem(shape, F32), vmem(shape, F32),
+        vmem(shape, F32),
         vmem((8, 2, 4, CY, CZ), F32),
-        vmem((8, 2, 64, CZ), F32), vmem((8, 2, 80, CZ), F32),
+        vmem((8, 2, 64, CZ), F32), vmem((8, 2, PIECES, 16 + PART, CZ), F32),
         vmem((8, 2, 16, CZ), F32), vmem((8, 2, 16, CZ), F32),
         pltpu.SemaphoreType.DMA((12,)),
-        pltpu.SemaphoreType.DMA((8, 6)), pltpu.SemaphoreType.DMA((8, 6)),
+        pltpu.SemaphoreType.DMA((8, 6, 3)), pltpu.SemaphoreType.DMA((8, 6, 3)),
     ]
     vmem_spec = pl.BlockSpec(memory_space=pltpu.VMEM)
     hbm_spec = pl.BlockSpec(memory_space=pltpu.HBM)

time: 30.9 us -> 29.2 us (0.945)
  Pallas kernels: 30 us -> 28.1 us
    pallas_call x1, Pallas kernels: 29.1 us -> 27.2 us  [local(): pl.pallas_call(kernel, out_shape=(vmem(shape, F32),) * 3, in_specs=[hbm_s...]
where the time goes in v3:
time: 29.2 us; the launch traced here: 28.8 us
  Pallas kernels  28.1 us (96%)
  between operations  0.64 us (2%)
    pallas_call x1, Pallas kernels, local(): pl.pallas_call(kernel, out_shape=(vmem(shape, F32),) * 3, in_specs=[hbm_s...  27.2 us
    pallas_call x1, Pallas kernels, local(): pl.pallas_call(put_out, out_shape=(block,) * 3, in_specs=[pl.BlockSpec(me...  0.9 us

profile of v3, /device:TPU:24, one launch (start us, length us, event | category | flops | bytes accessed | tf_op | source)
XLA Modules:
  0.0 28.8 jit_solution(11674738834287023267)
XLA Ops:
  0.6 27.2 %adjoint_window.1 = (f32[16,32,128]{2,1,0:T(8,128)S(1)}, f32[16,32,128]{2,1,0:T(8,128)S(1)}, f32[16,32,128]{2,1,0:T(8,128)S(1)}) custom-call(f32[4,16,32,128]{3,2,1,0:T(8,128)} %coef.1, s32[4,4,8,32]{3,2,1,0:T(8,128)} %keep.1, f32[16,32,128]{2,1,0:T(8,128)} %cour.1, f32[16,32,128]{2,1,0:T(8,128)} %damp.1, f32[16,32,128]{2,1,0:T(8,128)} %nxt.1, ...), custom_call_target="tpu_custom_call" | custom-call | tf_op jit(solution)/shard_map/adjoint_window/pallas_call | solution.py:435
  27.9 0.9 %put_out.1 = (f32[16,32,128]{2,1,0:T(8,128)}, f32[16,32,128]{2,1,0:T(8,128)}, f32[16,32,128]{2,1,0:T(8,128)}) custom-call(f32[16,32,128]{2,1,0:T(8,128)S(1)} %get-tuple-element.6.grad_v, f32[16,32,128]{2,1,0:T(8,128)S(1)} %get-tuple-element.7.last_v, f32[16,32,128]{2,1,0:T(8,128)S(1)} %get-tuple-element.8.before_v), custom_call_target="tpu_custom_call" | custom-call | tf_op jit(solution)/shard_map/put_out/pallas_call | solution.py:450

commit v4 on v3

--- a/solution.py
+++ b/solution.py
@@ -11,7 +11,7 @@
 STAR = (-205.0 / 72.0, 8.0 / 5.0, -1.0 / 5.0, 8.0 / 315.0, -1.0 / 560.0)
 CX, CY, CZ, STEPS, RECS = 16, 32, 128, 4, 128
 ROWS = CX * CY
-PIECES = 2
+PIECES = 4
 PART = 64 // PIECES
 AXES = ("gx", "gy", "gz")
 MESH = pl.DeviceIdType.MESH
@@ -33,13 +33,12 @@
     taps = np.select([gap == k for k in range(1, 5)], STAR[1:], 0.0)
     taps_hl = np.concatenate(split_np(taps), axis=1)
     z_hl = np.concatenate(split_np(along_z), axis=1)
-    mats = np.stack(
-        [np.concatenate([taps_hl, taps_hl]), np.concatenate([z_hl, z_hl])]
-    )
     decode_xy = np.concatenate(split_np(along_xy), axis=1)
-    spread_z = np.kron(np.eye(CZ // 4), np.ones((1, 4))).astype(jnp.bfloat16)
+    spread_z = np.kron(np.eye(CZ // 4), np.ones((1, 4)))
     spread_y = np.kron(np.eye(STEPS * CX // 4), np.kron(np.eye(CY // 4), np.ones((4, 1))))
-    return mats, decode_xy, spread_z, spread_y.astype(jnp.bfloat16)
+    spread = np.concatenate([spread_z, spread_y]).astype(jnp.bfloat16)
+    spread = np.pad(spread, ((0, 0), (0, CZ)))
+    return np.concatenate([taps_hl, taps_hl, z_hl, z_hl, decode_xy, spread])
 
 
 def split(value):
@@ -57,30 +56,16 @@
 
 
 def kernel(
-    coef, keep, cour, damp, nxt, now, cell, data, mats, dxy, spz, spy,
+    coef, keep, cour, damp, nxt, now, cell, data, ops,
     grad_o, last_o, before_o,
-    F, cin, kin, cour_v, damp_v, next_v, cell_v, data_v, mats_v, dxy_v, spz_v, spy_v,
+    F, cin, kin, edge_v, trio, cell_v, data_v, ops_v,
     wa, wb, we, inj, thr, Z, XH, YP, YH, ZP, ZH,
-    load_sem, send_sem, recv_sem,
+    load_sem, send_sem, step_sem, forward_sem,
 ):
     me = [lax.axis_index(axis) for axis in AXES]
     size = [lax.axis_size(axis) for axis in AXES]
     has = [(me[d] > 0, me[d] < size[d] - 1) for d in range(3)]
     other = [({AXES[d]: me[d] - 1}, {AXES[d]: me[d] + 1}) for d in range(3)]
-
-    loads = [
-        pltpu.make_async_copy(src, dst, load_sem.at[n])
-        for n, (src, dst) in enumerate(
-            [
-                (now, F.at[0, pl.ds(4, CX), pl.ds(8, CY)]),
-                (mats, mats_v), (keep, kin), (spz, spz_v), (spy, spy_v), (dxy, dxy_v),
-                (coef, cin), (damp, damp_v), (cour, cour_v), (nxt, next_v),
-                (cell, cell_v), (data, data_v),
-            ]
-        )
-    ]
-    for load in loads:
-        load.start()
 
     barrier = pltpu.get_barrier_semaphore()
     for d in range(3):
@@ -90,6 +75,18 @@
                 pl.semaphore_signal(
                     barrier, inc=1, device_id=other[d][side], device_id_type=MESH
                 )
+
+    def load(n, src, dst):
+        return pltpu.make_async_copy(src, dst, load_sem.at[n])
+
+    edges = [load(n, now.at[:, pl.ds(24 * n, 8)], edge_v.at[n]) for n in range(2)]
+    first = load(2, now, F.at[0, pl.ds(4, CX), pl.ds(8, CY)])
+    tables_in = [load(3, ops, ops_v), load(4, keep, kin), load(5, coef, cin)]
+    points_in = [load(7, cell, cell_v), load(8, data, data_v)]
+    fields_in = [load(6, src, trio.at[n]) for n, src in enumerate((cour, damp, nxt))]
+    cour_v, damp_v, next_v = (trio.at[n] for n in range(3))
+    for copy in edges + [first]:
+        copy.start()
 
     def clear(f, carry):
         F[f, 0:4] = jnp.zeros((4, 48, CZ), F32)
@@ -141,16 +138,27 @@
         else:
             pairs = [(ZP.at[f, side], ZH.at[f, 1 - side])]
         return [
-            pltpu.make_async_remote_copy(
-                src_ref=src,
-                dst_ref=dst,
-                send_sem=send_sem.at[f, 2 * d + side, n],
-                recv_sem=recv_sem.at[f, 2 * d + 1 - side, n],
-                device_id=other[d][side],
-                device_id_type=MESH,
-            )
+            copy_to(f, d, side, n if d == 1 else 0, src, dst)
             for n, (src, dst) in list(enumerate(pairs))[some]
         ]
+
+    def copy_to(f, d, side, n, src, dst):
+        if f < STEPS:
+            landed = step_sem.at[f % 2, 1 - side, (0, 2 + n, 1)[d]]
+        else:
+            landed = forward_sem.at[f - STEPS, d, 1 - side]
+        return pltpu.make_async_remote_copy(
+            src_ref=src,
+            dst_ref=dst,
+            send_sem=send_sem.at[d, side],
+            recv_sem=landed,
+            device_id=other[d][side],
+            device_id_type=MESH,
+        )
+
+    def whole(f, d, side):
+        from_ref, to_ref = ((XH, XH), (YP, YP), (ZP, ZH))[d]
+        return copy_to(f, d, side, 0, from_ref.at[f, side], to_ref.at[f, 1 - side])
 
     def each_side(d, act):
         for side in range(2):
@@ -161,11 +169,18 @@
     def send(f, d, some=slice(None)):
         each_side(d, lambda side: [copy.start() for copy in faces(f, d, side, some)])
 
-    def arrive(f, d, some=slice(None)):
-        each_side(d, lambda side: [copy.wait_recv() for copy in faces(f, d, 1 - side, some)])
-
-    def drain(f, d):
-        each_side(d, lambda side: [copy.wait_send() for copy in faces(f, d, side)])
+    def arrive(f, d, piece=None):
+        if piece is None:
+            each_side(d, lambda side: whole(f, d, 1 - side).wait_recv())
+        else:
+            some = slice(piece, piece + 1)
+            each_side(d, lambda side: [copy.wait_recv() for copy in faces(f, d, 1 - side, some)])
+
+    def drain(d):
+        every = (XH, YP, ZP)[d]
+        each_side(
+            d, lambda side: copy_to(0, d, side, 0, every.at[:, side], every.at[:, side]).wait_send()
+        )
 
     def pack_rows(f):
         def pack_y(p, carry):
@@ -198,7 +213,7 @@
 
     def own_z(f):
         value = F[f, 4:20, 8:40, :].reshape(ROWS, CZ)
-        return halves(dot(jnp.concatenate(split(value), axis=1), mats_v[0]))
+        return halves(dot(jnp.concatenate(split(value), axis=1), ops_v[0:256]))
 
     def far_z(f):
         member = lane % 4
@@ -281,7 +296,7 @@
         if sends:
             send(s + 1, 0, slice(0, 1))
         for piece in range(PIECES):
-            arrive(s, 1, slice(piece, piece + 1))
+            arrive(s, 1, piece)
             for p in range(8 * piece // PIECES, 8 * (piece + 1) // PIECES):
                 lows, highs = [], []
                 for x in (2 * p, 2 * p + 1):
@@ -311,10 +326,10 @@
             jnp.where(level + float(x % 4) < thr[s, x // 4], cin[s, x], 0.0) for x in range(CX)
         ]
         value = jnp.concatenate(masked, axis=0)
-        along_z = halves(dot(jnp.concatenate(split(value), axis=1), mats_v[1]))
+        along_z = halves(dot(jnp.concatenate(split(value), axis=1), ops_v[256:512]))
         for g in range(CX // 4):
             both = jnp.concatenate(split(along_z[CZ * g : CZ * g + CZ]), axis=1)
-            out = halves(dot(dxy_v[...], jnp.concatenate([both, both], axis=0)))
+            out = halves(dot(ops_v[512:640], jnp.concatenate([both, both], axis=0)))
             F[4 + s, 4 + 4 * g : 8 + 4 * g, 8:40, :] = out.reshape(4, CY, CZ)
 
     def gradient(s):
@@ -344,24 +359,33 @@
         for d in (1, 0, 2):
             send(4 + s, d)
 
-    loads[0].wait()
-    pack_rows(0)
-    pack_lanes(0)
+    for copy in edges:
+        copy.wait()
+    for copy in tables_in + fields_in + points_in:
+        copy.start()
+    for p in range(8):
+        for side in range(2):
+            two = [edge_v[side, 2 * p + q, 4 * side : 4 * side + 4, :] for q in range(2)]
+            YP[0, side, 8 * p : 8 * p + 8, :] = jnp.concatenate(two, axis=0)
     peers = sum(there.astype(jnp.int32) for pair in has for there in pair)
     pl.semaphore_wait(barrier, peers)
-    for d in (1, 0, 2):
-        send(0, d)
-
-    for load in loads[1:7]:
-        load.wait()
+    send(0, 1)
+    first.wait()
+    send(0, 0)
+    pack_lanes(0)
+    send(0, 2)
+
+    for copy in tables_in:
+        copy.wait()
     levels = kin[...].reshape(STEPS * (CX // 4) * (CY // 4), CZ // 4).astype(F32).astype(BF16)
-    wide = dot(levels, spz_v[...]).astype(BF16)
-    thr[...] = dot(spy_v[...], wide).reshape(STEPS, CX // 4, CY, CZ)
+    wide = dot(levels, ops_v[640:672, 0:CZ]).astype(BF16)
+    thr[...] = jnp.concatenate([dot(ops_v[672 + 256 * h : 928 + 256 * h, 0:CZ], wide) for h in range(2)]).reshape(STEPS, CX // 4, CY, CZ)
     for s in range(2):
         send_forward(s)
 
-    for load in loads[7:]:
-        load.wait()
+    load(6, trio, trio).wait()
+    for copy in points_in:
+        copy.wait()
 
     def weights(x, carry):
         over = 1.0 / (1.0 + damp_v[x])
@@ -394,9 +418,8 @@
             gradient(s)
             if s == STEPS - 2:
                 gradient(s + 1)
-    for f in range(2 * STEPS):
-        for d in range(3):
-            drain(f, d)
+    for d in range(3):
+        drain(d)
 
 
 def put_out(grad_v, last_v, before_v, grad_o, last_o, before_o, sem):
@@ -411,15 +434,14 @@
 def local(coef, keep, courant, damp, adj_next, adj_now, rec_cell, rec_data):
     shape = (CX, CY, CZ)
     block = jax.ShapeDtypeStruct(shape, F32)
-    mats, dxy, spz, spy = tables()
+    ops = tables()
     vmem = pltpu.VMEM
     scratch = [
         vmem((8, 24, 48, CZ), F32),
         vmem((STEPS,) + shape, F32),
         vmem((STEPS, CX // 4, CY // 4, CZ // 4), jnp.int32),
-        vmem(shape, F32), vmem(shape, F32), vmem(shape, F32),
-        vmem((1, RECS), jnp.int32), vmem((STEPS, RECS), F32),
-        vmem(mats.shape, BF16), vmem(dxy.shape, BF16), vmem(spz.shape, BF16), vmem(spy.shape, BF16),
+        vmem((2, CX, 8, CZ), F32), vmem((3,) + shape, F32),
+        vmem((1, RECS), jnp.int32), vmem((STEPS, RECS), F32), vmem(ops.shape, BF16),
         vmem(shape, F32), vmem(shape, F32), vmem(shape, F32),
         vmem((STEPS,) + shape, F32),
         vmem((STEPS, CX // 4, CY, CZ), F32),
@@ -427,15 +449,16 @@
         vmem((8, 2, 4, CY, CZ), F32),
         vmem((8, 2, 64, CZ), F32), vmem((8, 2, PIECES, 16 + PART, CZ), F32),
         vmem((8, 2, 16, CZ), F32), vmem((8, 2, 16, CZ), F32),
-        pltpu.SemaphoreType.DMA((12,)),
-        pltpu.SemaphoreType.DMA((8, 6, 3)), pltpu.SemaphoreType.DMA((8, 6, 3)),
+        pltpu.SemaphoreType.DMA((9,)),
+        pltpu.SemaphoreType.DMA((3, 2)), pltpu.SemaphoreType.DMA((2, 2, 2 + PIECES)),
+        pltpu.SemaphoreType.DMA((STEPS, 3, 2)),
     ]
     vmem_spec = pl.BlockSpec(memory_space=pltpu.VMEM)
     hbm_spec = pl.BlockSpec(memory_space=pltpu.HBM)
     results = pl.pallas_call(
         kernel,
         out_shape=(vmem(shape, F32),) * 3,
-        in_specs=[hbm_spec] * 12,
+        in_specs=[hbm_spec] * 9,
         out_specs=(vmem_spec,) * 3,
         scratch_shapes=scratch,
         compiler_params=pltpu.CompilerParams(
@@ -445,7 +468,7 @@
     )(
         coef, keep, courant, damp, adj_next, adj_now,
         rec_cell.reshape(1, RECS), rec_data.reshape(STEPS, RECS),
-        jnp.asarray(mats), jnp.asarray(dxy), jnp.asarray(spz), jnp.asarray(spy),
+        jnp.asarray(ops),
     )
     return pl.pallas_call(
         put_out,

time: 29.2 us -> 27.2 us (0.932)
  Pallas kernels: 28.1 us -> 26.1 us
    pallas_call x1, Pallas kernels: 27.2 us -> 25.2 us  [local(): pl.pallas_call(kernel, out_shape=(vmem(shape, F32),) * 3, in_specs=[hbm_s...]
where the time goes in v4:
time: 27.2 us; the launch traced here: 26.7 us
  Pallas kernels  26.1 us (96%)
  between operations  0.64 us (2%)
    pallas_call x1, Pallas kernels, local(): pl.pallas_call(kernel, out_shape=(vmem(shape, F32),) * 3, in_specs=[hbm_s...  25.2 us
    pallas_call x1, Pallas kernels, local(): pl.pallas_call(put_out, out_shape=(block,) * 3, in_specs=[pl.BlockSpec(me...  0.9 us

profile of v4, /device:TPU:24, one launch (start us, length us, event | category | flops | bytes accessed | tf_op | source)
XLA Modules:
  0.0 26.7 jit_solution(10331822027047167705)
XLA Ops:
  0.6 25.2 %adjoint_window.1 = (f32[16,32,128]{2,1,0:T(8,128)S(1)}, f32[16,32,128]{2,1,0:T(8,128)S(1)}, f32[16,32,128]{2,1,0:T(8,128)S(1)}) custom-call(f32[4,16,32,128]{3,2,1,0:T(8,128)} %coef.1, s32[4,4,8,32]{3,2,1,0:T(8,128)} %keep.1, f32[16,32,128]{2,1,0:T(8,128)} %cour.1, f32[16,32,128]{2,1,0:T(8,128)} %damp.1, f32[16,32,128]{2,1,0:T(8,128)} %nxt.1, ...), custom_call_target="tpu_custom_call" | custom-call | tf_op jit(solution)/shard_map/adjoint_window/pallas_call | solution.py:458
  25.8 0.9 %put_out.1 = (f32[16,32,128]{2,1,0:T(8,128)}, f32[16,32,128]{2,1,0:T(8,128)}, f32[16,32,128]{2,1,0:T(8,128)}) custom-call(f32[16,32,128]{2,1,0:T(8,128)S(1)} %get-tuple-element.6.grad_v, f32[16,32,128]{2,1,0:T(8,128)S(1)} %get-tuple-element.7.last_v, f32[16,32,128]{2,1,0:T(8,128)S(1)} %get-tuple-element.8.before_v), custom_call_target="tpu_custom_call" | custom-call | tf_op jit(solution)/shard_map/put_out/pallas_call | solution.py:473

commit v5 on v4

--- a/solution.py
+++ b/solution.py
@@ -11,8 +11,7 @@
 STAR = (-205.0 / 72.0, 8.0 / 5.0, -1.0 / 5.0, 8.0 / 315.0, -1.0 / 560.0)
 CX, CY, CZ, STEPS, RECS = 16, 32, 128, 4, 128
 ROWS = CX * CY
-PIECES = 4
-PART = 64 // PIECES
+UNROLL = 16
 AXES = ("gx", "gy", "gz")
 MESH = pl.DeviceIdType.MESH
 F32, BF16 = jnp.float32, jnp.bfloat16
@@ -59,8 +58,8 @@
     coef, keep, cour, damp, nxt, now, cell, data, ops,
     grad_o, last_o, before_o,
     F, cin, kin, edge_v, trio, cell_v, data_v, ops_v,
-    wa, wb, we, inj, thr, Z, XH, YP, YH, ZP, ZH,
-    load_sem, send_sem, step_sem, forward_sem,
+    wa, wb, we, inj, thr, Z, XH, YP, YH, CP, XC, ZP, ZH,
+    load_sem, send_sem, step_sem, row_sem, forward_sem,
 ):
     me = [lax.axis_index(axis) for axis in AXES]
     size = [lax.axis_size(axis) for axis in AXES]
@@ -94,9 +93,8 @@
         F[f, 4:20, 0:8] = jnp.zeros((CX, 8, CZ), F32)
         F[f, 4:20, 40:48] = jnp.zeros((CX, 8, CZ), F32)
         for side in range(2):
-            for n in range(PIECES):
-                YH[f, side, n, 0:8] = jnp.zeros((8, CZ), F32)
-                YH[f, side, n, 8 + PART : 16 + PART] = jnp.zeros((8, CZ), F32)
+            YH[f, side, 0:8] = jnp.zeros((8, CZ), F32)
+            YH[f, side, 72:80] = jnp.zeros((8, CZ), F32)
 
             @pl.when(jnp.logical_not(has[0][side]))
             def _():
@@ -104,7 +102,7 @@
 
             @pl.when(jnp.logical_not(has[1][side]))
             def _():
-                YH[f, side, :, 8 : 8 + PART] = jnp.zeros((PIECES, PART, CZ), F32)
+                YH[f, side, 8:72] = jnp.zeros((64, CZ), F32)
 
             @pl.when(jnp.logical_not(has[2][side]))
             def _():
@@ -113,10 +111,22 @@
         return carry
 
     lax.fori_loop(0, 8, clear, 0)
+    for side in range(2):
+        for f in range(STEPS - 1):
+            CP[f, side, 0:8] = jnp.zeros((8, CZ), F32)
+            CP[f, side, 72:80] = jnp.zeros((8, CZ), F32)
+
+        @pl.when(jnp.logical_not(has[1][side]))
+        def _():
+            YH[8, side, 8:72] = jnp.zeros((64, CZ), F32)
 
     lane = lax.broadcasted_iota(jnp.int32, (8, CZ), 1)
     sub = lax.broadcasted_iota(jnp.int32, (8, CZ), 0)
     near_low = [None] + [jnp.where(sub < k, STAR[k], 0.0).astype(F32) for k in range(1, 5)]
+    across = [
+        [None] + [jnp.where(sub % 4 >= 4 - k, STAR[k], 0.0).astype(F32) for k in range(1, 5)],
+        [None] + [jnp.where(sub % 4 < k, STAR[k], 0.0).astype(F32) for k in range(1, 5)],
+    ]
     near_high = [None] + [jnp.where(sub >= 8 - k, STAR[k], 0.0).astype(F32) for k in range(1, 5)]
 
     def faces(f, d, side, some=slice(None)):
@@ -132,21 +142,22 @@
             ]
         elif d == 1:
             pairs = [
-                (YP.at[f, side, pl.ds(PART * n, PART)], YH.at[f, 1 - side, n, pl.ds(8, PART)])
-                for n in range(PIECES)
+                (YP.at[f, side, pl.ds(row, 16)], YH.at[f, 1 - side, pl.ds(8 + row, 16)])
+                for row in range(0, 64, 16)
             ]
         else:
             pairs = [(ZP.at[f, side], ZH.at[f, 1 - side])]
         return [
-            copy_to(f, d, side, n if d == 1 else 0, src, dst)
-            for n, (src, dst) in list(enumerate(pairs))[some]
+            copy_to(f, d, side, src, dst) for src, dst in pairs[some]
         ]
 
-    def copy_to(f, d, side, n, src, dst):
-        if f < STEPS:
-            landed = step_sem.at[f % 2, 1 - side, (0, 2 + n, 1)[d]]
+    def copy_to(f, d, side, src, dst):
+        if d == 1:
+            landed = row_sem.at[f, 1 - side]
+        elif f < STEPS:
+            landed = step_sem.at[f % 2, d // 2, 1 - side]
         else:
-            landed = forward_sem.at[f - STEPS, d, 1 - side]
+            landed = forward_sem.at[f - STEPS, d // 2, 1 - side]
         return pltpu.make_async_remote_copy(
             src_ref=src,
             dst_ref=dst,
@@ -158,7 +169,7 @@
 
     def whole(f, d, side):
         from_ref, to_ref = ((XH, XH), (YP, YP), (ZP, ZH))[d]
-        return copy_to(f, d, side, 0, from_ref.at[f, side], to_ref.at[f, 1 - side])
+        return copy_to(f, d, side, from_ref.at[f, side], to_ref.at[f, 1 - side])
 
     def each_side(d, act):
         for side in range(2):
@@ -169,17 +180,13 @@
     def send(f, d, some=slice(None)):
         each_side(d, lambda side: [copy.start() for copy in faces(f, d, side, some)])
 
-    def arrive(f, d, piece=None):
-        if piece is None:
-            each_side(d, lambda side: whole(f, d, 1 - side).wait_recv())
-        else:
-            some = slice(piece, piece + 1)
-            each_side(d, lambda side: [copy.wait_recv() for copy in faces(f, d, 1 - side, some)])
+    def arrive(f, d):
+        each_side(d, lambda side: whole(f, d, 1 - side).wait_recv())
 
     def drain(d):
         every = (XH, YP, ZP)[d]
         each_side(
-            d, lambda side: copy_to(0, d, side, 0, every.at[:, side], every.at[:, side]).wait_send()
+            d, lambda side: copy_to(0, d, side, every.at[:, side], every.at[:, side]).wait_send()
         )
 
     def pack_rows(f):
@@ -242,23 +249,20 @@
             high = pltpu.roll(packed[half][1], (252 - 4 * i) % CZ, 1)
             value = jnp.where(lane < 4, low, jnp.where(lane >= CZ - 4, high, 0.0))
             x, row = v // 4, 8 * (v % 4)
-            if scale is not None:
-                value = scale[x, row : row + 8] * value
-            target[x, row : row + 8] = target[x, row : row + 8] + value
+            at = (x, slice(row, row + 8))
+            target[at] = target[at] + scale(*at) * value
 
     def add_x(f, target, scale):
         for i in range(4):
             low = sum(STAR[k] * XH[f, 0, 4 + i - k] for k in range(i + 1, 5))
             high = sum(STAR[4 + m - i] * XH[f, 1, m] for m in range(i + 1))
-            if scale is not None:
-                low, high = scale[i] * low, scale[12 + i] * high
-            target[i] = target[i] + low
-            target[12 + i] = target[12 + i] + high
+            target[i] = target[i] + scale(i) * low
+            target[12 + i] = target[12 + i] + scale(12 + i) * high
 
     def near_y(f, x):
-        n, at = divmod(4 * x, PART)
-        low = sum(near_low[k] * YH[f, 0, n, 12 + at - k : 20 + at - k] for k in range(1, 5))
-        high = sum(near_high[k] * YH[f, 1, n, at + k : at + k + 8] for k in range(1, 5))
+        at = 4 * x
+        low = sum(near_low[k] * YH[f, 0, 12 + at - k : 20 + at - k] for k in range(1, 5))
+        high = sum(near_high[k] * YH[f, 1, at + k : at + k + 8] for k in range(1, 5))
         return low, high
 
     def own_star(f, x):
@@ -284,34 +288,65 @@
                 before_o[x] = current
             return carry
 
-        lax.fori_loop(0, CX, step, 0, unroll=2)
-
-    def adjoint_far(s):
+        lax.fori_loop(0, CX, step, 0, unroll=UNROLL)
+
+    def send_partial(f, pieces):
+        target = target_of(f - 1)
+        for n in pieces:
+            for p in (2 * n, 2 * n + 1):
+                for side, row in ((0, 0), (1, 28)):
+                    two = [target[2 * p + q, row : row + 4, :] for q in range(2)]
+                    YP[f, side, 8 * p : 8 * p + 8] = jnp.concatenate(two, axis=0)
+        for n in pieces:
+            send(f, 1, slice(n, n + 1))
+
+    def step_scale(*at):
+        return we[at]
+
+    def adjoint_near(s):
         target = target_of(s)
         sends = s < STEPS - 1
         arrive(s, 2)
-        add_z(s, target, we)
+        add_z(s, target, step_scale)
+        if sends:
+            send_partial(s + 1, (1, 2))
         arrive(s, 0)
-        add_x(s, target, we)
+        add_x(s, target, step_scale)
         if sends:
+            send_partial(s + 1, (0, 3))
             send(s + 1, 0, slice(0, 1))
-        for piece in range(PIECES):
-            arrive(s, 1, piece)
-            for p in range(8 * piece // PIECES, 8 * (piece + 1) // PIECES):
-                lows, highs = [], []
-                for x in (2 * p, 2 * p + 1):
-                    low, high = near_y(s, x)
-                    low = target[x, 0:8] + we[x, 0:8] * low
-                    high = target[x, 24:32] + we[x, 24:32] * high
-                    lows.append(low[0:4])
-                    highs.append(high[4:8])
-                    target[x, 0:8] = low
-                    target[x, 24:32] = high
-                if sends:
-                    YP[s + 1, 0, 8 * p : 8 * p + 8] = jnp.concatenate(lows, axis=0)
-                    YP[s + 1, 1, 8 * p : 8 * p + 8] = jnp.concatenate(highs, axis=0)
-            if sends:
-                send(s + 1, 1, slice(piece, piece + 1))
+
+    def cross(f):
+        for p in range(8):
+            at = 8 + 8 * p
+            for side in range(2):
+                total = 0.0
+                for k in range(1, 5):
+                    move = k - 4 if side == 0 else 4 - k
+                    part = CP[f - 1, side, at + move : at + move + 8]
+                    total = total + across[side][k] * part
+                XC[side, 8 * p : 8 * p + 8] = YH[8, side, at : at + 8] * total
+
+    def adjoint_rows(s):
+        target = target_of(s)
+        sends = s < STEPS - 1
+        arrive(s, 1)
+        if s > 0:
+            for side in range(2):
+                YH[s, side, 8:72] = YH[s, side, 8:72] + XC[side]
+        for p in range(8):
+            lows, highs = [], []
+            for x in (2 * p, 2 * p + 1):
+                low, high = near_y(s, x)
+                low = target[x, 0:8] + we[x, 0:8] * low
+                high = target[x, 24:32] + we[x, 24:32] * high
+                lows.append(low[0:4])
+                highs.append(high[4:8])
+                target[x, 0:8] = low
+                target[x, 24:32] = high
+            if s < STEPS - 2:
+                CP[s + 1, 0, 8 + 8 * p : 16 + 8 * p] = jnp.concatenate(lows, axis=0)
+                CP[s + 1, 1, 8 + 8 * p : 16 + 8 * p] = jnp.concatenate(highs, axis=0)
         if sends:
             send(s + 1, 0, slice(1, 3))
             pack_lanes(s + 1)
@@ -332,30 +367,40 @@
             out = halves(dot(ops_v[512:640], jnp.concatenate([both, both], axis=0)))
             F[4 + s, 4 + 4 * g : 8 + 4 * g, 8:40, :] = out.reshape(4, CY, CZ)
 
-    def gradient(s):
+    def gradient_own(s):
+        Z[...] = own_z(4 + s).reshape(CX, CY, CZ)
+
+        def step(x, carry):
+            value = cour_v[x] * F[s, 4 + x, 8:40, :] * own_star(4 + s, x)
+            grad_o[x] = value if s == 0 else grad_o[x] + value
+            return carry
+
+        lax.fori_loop(0, CX, step, 0, unroll=UNROLL)
+
+    def gradient_far(s):
         f = 4 + s
-        Z[...] = own_z(f).reshape(CX, CY, CZ)
+        current = F.at[s, pl.ds(4, CX), pl.ds(8, CY)]
+
+        def scale(*at):
+            return cour_v[at] * current[at]
+
         arrive(f, 2)
-        add_z(f, Z, None)
+        add_z(f, grad_o, scale)
         arrive(f, 0)
-        add_x(f, Z, None)
+        add_x(f, grad_o, scale)
         arrive(f, 1)
         for x in range(CX):
             low, high = near_y(f, x)
-            Z[x, 0:8] = Z[x, 0:8] + low
-            Z[x, 24:32] = Z[x, 24:32] + high
-
-        def step(x, carry):
-            value = cour_v[x] * F[s, 4 + x, 8:40, :] * own_star(f, x)
-            grad_o[x] = value if s == 0 else grad_o[x] + value
-            return carry
-
-        lax.fori_loop(0, CX, step, 0, unroll=2)
-
-    def send_forward(s):
+            top, end = slice(0, 8), slice(24, 32)
+            grad_o[x, top] = grad_o[x, top] + scale(x, top) * low
+            grad_o[x, end] = grad_o[x, end] + scale(x, end) * high
+
+    def prepare(s):
         decode(s)
         pack_rows(4 + s)
         pack_lanes(4 + s)
+
+    def post(s):
         for d in (1, 0, 2):
             send(4 + s, d)
 
@@ -366,7 +411,9 @@
     for p in range(8):
         for side in range(2):
             two = [edge_v[side, 2 * p + q, 4 * side : 4 * side + 4, :] for q in range(2)]
-            YP[0, side, 8 * p : 8 * p + 8, :] = jnp.concatenate(two, axis=0)
+            rows = jnp.concatenate(two, axis=0)
+            YP[0, side, 8 * p : 8 * p + 8, :] = rows
+            CP[0, side, 8 + 8 * p : 16 + 8 * p, :] = rows
     peers = sum(there.astype(jnp.int32) for pair in has for there in pair)
     pl.semaphore_wait(barrier, peers)
     send(0, 1)
@@ -375,14 +422,6 @@
     pack_lanes(0)
     send(0, 2)
 
-    for copy in tables_in:
-        copy.wait()
-    levels = kin[...].reshape(STEPS * (CX // 4) * (CY // 4), CZ // 4).astype(F32).astype(BF16)
-    wide = dot(levels, ops_v[640:672, 0:CZ]).astype(BF16)
-    thr[...] = jnp.concatenate([dot(ops_v[672 + 256 * h : 928 + 256 * h, 0:CZ], wide) for h in range(2)]).reshape(STEPS, CX // 4, CY, CZ)
-    for s in range(2):
-        send_forward(s)
-
     load(6, trio, trio).wait()
     for copy in points_in:
         copy.wait()
@@ -395,6 +434,13 @@
         return carry
 
     lax.fori_loop(0, CX, weights, 0, unroll=2)
+
+    for p in range(8):
+        for side in range(2):
+            row = 28 * side
+            two = [we[2 * p + q, row : row + 4, :] for q in range(2)]
+            YP[8, side, 8 * p : 8 * p + 8] = jnp.concatenate(two, axis=0)
+    send(8, 1)
 
     row = lax.broadcasted_iota(jnp.int32, (ROWS, RECS), 0)
     rows_hot = jnp.where(row == cell_v[...] // CZ, 1.0, 0.0).astype(BF16)
@@ -408,16 +454,47 @@
         )
         inj[s] = spread.reshape(CX, CY, CZ) * (0.5 * wa[...])
 
+    for copy in tables_in:
+        copy.wait()
+    levels = kin[...].reshape(STEPS * (CX // 4) * (CY // 4), CZ // 4).astype(F32).astype(BF16)
+    wide = dot(levels, ops_v[640:672, 0:CZ]).astype(BF16)
+    thr[...] = jnp.concatenate([dot(ops_v[672 + 256 * h : 928 + 256 * h, 0:CZ], wide) for h in range(2)]).reshape(STEPS, CX // 4, CY, CZ)
+
+    prepare(0)
+    post(0)
     adjoint_own(0)
-    for s in range(STEPS):
-        adjoint_far(s)
-        if s < STEPS - 1:
-            if s < 2:
-                send_forward(2 + s)
-            adjoint_own(s + 1)
-            gradient(s)
-            if s == STEPS - 2:
-                gradient(s + 1)
+    prepare(1)
+    adjoint_near(0)
+    adjoint_rows(0)
+    post(1)
+    arrive(8, 1)
+
+    adjoint_own(1)
+    cross(1)
+    prepare(2)
+    gradient_own(0)
+    adjoint_near(1)
+    adjoint_rows(1)
+    post(2)
+
+    adjoint_own(2)
+    cross(2)
+    prepare(3)
+    post(3)
+    gradient_own(1)
+    gradient_far(0)
+    adjoint_near(2)
+    adjoint_rows(2)
+
+    adjoint_own(3)
+    cross(3)
+    gradient_own(2)
+    gradient_own(3)
+    gradient_far(1)
+    gradient_far(2)
+    adjoint_near(3)
+    gradient_far(3)
+    adjoint_rows(3)
     for d in range(3):
         drain(d)
 
@@ -447,11 +524,12 @@
         vmem((STEPS, CX // 4, CY, CZ), F32),
         vmem(shape, F32),
         vmem((8, 2, 4, CY, CZ), F32),
-        vmem((8, 2, 64, CZ), F32), vmem((8, 2, PIECES, 16 + PART, CZ), F32),
+        vmem((9, 2, 64, CZ), F32), vmem((9, 2, 80, CZ), F32),
+        vmem((STEPS - 1, 2, 80, CZ), F32), vmem((2, 64, CZ), F32),
         vmem((8, 2, 16, CZ), F32), vmem((8, 2, 16, CZ), F32),
         pltpu.SemaphoreType.DMA((9,)),
-        pltpu.SemaphoreType.DMA((3, 2)), pltpu.SemaphoreType.DMA((2, 2, 2 + PIECES)),
-        pltpu.SemaphoreType.DMA((STEPS, 3, 2)),
+        pltpu.SemaphoreType.DMA((3, 2)), pltpu.SemaphoreType.DMA((2, 2, 2)),
+        pltpu.SemaphoreType.DMA((9, 2)), pltpu.SemaphoreType.DMA((STEPS, 2, 2)),
     ]
     vmem_spec = pl.BlockSpec(memory_space=pltpu.VMEM)
     hbm_spec = pl.BlockSpec(memory_space=pltpu.HBM)

time: 27.2 us -> 26.3 us (0.967); the launches traced: 26.7 us -> 26.2 us
  Pallas kernels: 26.1 us -> 25.6 us
    pallas_call x1, Pallas kernels: 25.2 us -> 24.7 us  [local(): pl.pallas_call(kernel, out_shape=(vmem(shape, F32),) * 3, in_specs=[hbm_s...]
where the time goes in v5:
time: 26.3 us; the launch traced here: 26.2 us
  Pallas kernels  25.6 us (97%)
  between operations  0.64 us (2%)
    pallas_call x1, Pallas kernels, local(): pl.pallas_call(kernel, out_shape=(vmem(shape, F32),) * 3, in_specs=[hbm_s...  24.7 us
    pallas_call x1, Pallas kernels, local(): pl.pallas_call(put_out, out_shape=(block,) * 3, in_specs=[pl.BlockSpec(me...  0.9 us

profile of v5, /device:TPU:24, one launch (start us, length us, event | category | flops | bytes accessed | tf_op | source)
XLA Modules:
  0.0 26.2 jit_solution(5983877102659789939)
XLA Ops:
  0.6 24.7 %adjoint_window.1 = (f32[16,32,128]{2,1,0:T(8,128)S(1)}, f32[16,32,128]{2,1,0:T(8,128)S(1)}, f32[16,32,128]{2,1,0:T(8,128)S(1)}) custom-call(f32[4,16,32,128]{3,2,1,0:T(8,128)} %coef.1, s32[4,4,8,32]{3,2,1,0:T(8,128)} %keep.1, f32[16,32,128]{2,1,0:T(8,128)} %cour.1, f32[16,32,128]{2,1,0:T(8,128)} %damp.1, f32[16,32,128]{2,1,0:T(8,128)} %nxt.1, ...), custom_call_target="tpu_custom_call" | custom-call | tf_op jit(solution)/shard_map/adjoint_window/pallas_call | solution.py:536
  25.3 0.9 %put_out.1 = (f32[16,32,128]{2,1,0:T(8,128)}, f32[16,32,128]{2,1,0:T(8,128)}, f32[16,32,128]{2,1,0:T(8,128)}) custom-call(f32[16,32,128]{2,1,0:T(8,128)S(1)} %get-tuple-element.6.grad_v, f32[16,32,128]{2,1,0:T(8,128)S(1)} %get-tuple-element.7.last_v, f32[16,32,128]{2,1,0:T(8,128)S(1)} %get-tuple-element.8.before_v), custom_call_target="tpu_custom_call" | custom-call | tf_op jit(solution)/shard_map/put_out/pallas_call | solution.py:551

commit v6 on v5

--- a/solution.py
+++ b/solution.py
@@ -58,8 +58,8 @@
     coef, keep, cour, damp, nxt, now, cell, data, ops,
     grad_o, last_o, before_o,
     F, cin, kin, edge_v, trio, cell_v, data_v, ops_v,
-    wa, wb, we, inj, thr, Z, XH, YP, YH, CP, XC, ZP, ZH,
-    load_sem, send_sem, step_sem, row_sem, forward_sem,
+    wa, wb, we, inj, thr, Z, XH, YP, YH, CP, XC, XP, XM, XL, XT, ZP, ZH,
+    load_sem, send_sem, step_sem, row_sem, forward_sem, edge_sem,
 ):
     me = [lax.axis_index(axis) for axis in AXES]
     size = [lax.axis_size(axis) for axis in AXES]
@@ -67,7 +67,7 @@
     other = [({AXES[d]: me[d] - 1}, {AXES[d]: me[d] + 1}) for d in range(3)]
 
     barrier = pltpu.get_barrier_semaphore()
-    for d in range(3):
+    for d in (1, 0, 2):
         for side in range(2):
             @pl.when(has[d][side])
             def _():
@@ -112,7 +112,11 @@
 
     lax.fori_loop(0, 8, clear, 0)
     for side in range(2):
-        for f in range(STEPS - 1):
+        XT[side] = jnp.zeros((4, 16, CZ), F32)
+        for f in range(1, STEPS):
+            for row in (0, 24):
+                XH[f, side, :, row : row + 8] = jnp.zeros((4, 8, CZ), F32)
+        for f in range(STEPS):
             CP[f, side, 0:8] = jnp.zeros((8, CZ), F32)
             CP[f, side, 72:80] = jnp.zeros((8, CZ), F32)
 
@@ -130,16 +134,15 @@
     near_high = [None] + [jnp.where(sub >= 8 - k, STAR[k], 0.0).astype(F32) for k in range(1, 5)]
 
     def faces(f, d, side, some=slice(None)):
-        if d == 0:
+        if d == 0 and 0 < f < STEPS:
+            inner, there = pl.ds(8, 16), 1 - side
+            pairs = [(F.at[f, pl.ds(4 + 12 * side, 4), pl.ds(16, 16)], XH.at[f, there, :, inner])]
+            pairs += [(XP.at[f - 1, side, t], XM.at[f - 1, there, t]) for t in range(2)]
+            row = pl.ds(8 + 48 * side, 16)
+            pairs += [(CP.at[f, t, row], XL.at[f - 1, there, t]) for t in range(2)]
+        elif d == 0:
             start = 4 if side == 0 else CX
-            rows = ((8, 16), (0, 8), (24, 8)) if f < STEPS else ((0, CY),)
-            pairs = [
-                (
-                    F.at[f, pl.ds(start, 4), pl.ds(8 + row, count)],
-                    XH.at[f, 1 - side, slice(None), pl.ds(row, count)],
-                )
-                for row, count in rows
-            ]
+            pairs = [(F.at[f, pl.ds(start, 4), pl.ds(8, CY)], XH.at[f, 1 - side])]
         elif d == 1:
             pairs = [
                 (YP.at[f, side, pl.ds(row, 16)], YH.at[f, 1 - side, pl.ds(8 + row, 16)])
@@ -148,11 +151,13 @@
         else:
             pairs = [(ZP.at[f, side], ZH.at[f, 1 - side])]
         return [
-            copy_to(f, d, side, src, dst) for src, dst in pairs[some]
+            copy_to(f, d, side, src, dst, n) for n, (src, dst) in list(enumerate(pairs))[some]
         ]
 
-    def copy_to(f, d, side, src, dst):
-        if d == 1:
+    def copy_to(f, d, side, src, dst, n=0):
+        if d == 0 and n > 2:
+            landed = edge_sem.at[f % 2, 1 - side]
+        elif d == 1:
             landed = row_sem.at[f, 1 - side]
         elif f < STEPS:
             landed = step_sem.at[f % 2, d // 2, 1 - side]
@@ -167,9 +172,12 @@
             device_id_type=MESH,
         )
 
-    def whole(f, d, side):
+    def whole(f, d, side, n=0):
         from_ref, to_ref = ((XH, XH), (YP, YP), (ZP, ZH))[d]
-        return copy_to(f, d, side, from_ref.at[f, side], to_ref.at[f, 1 - side])
+        src, dst = from_ref.at[f, side], to_ref.at[f, 1 - side]
+        if d == 0 and 0 < f < STEPS:
+            src, dst = (ref.at[:, pl.ds(0, 8 if n else 24)] for ref in (src, dst))
+        return copy_to(f, d, side, src, dst, n)
 
     def each_side(d, act):
         for side in range(2):
@@ -180,8 +188,8 @@
     def send(f, d, some=slice(None)):
         each_side(d, lambda side: [copy.start() for copy in faces(f, d, side, some)])
 
-    def arrive(f, d):
-        each_side(d, lambda side: whole(f, d, 1 - side).wait_recv())
+    def arrive(f, d, n=0):
+        each_side(d, lambda side: whole(f, d, 1 - side, n).wait_recv())
 
     def drain(d):
         every = (XH, YP, ZP)[d]
@@ -252,12 +260,14 @@
             at = (x, slice(row, row + 8))
             target[at] = target[at] + scale(*at) * value
 
-    def add_x(f, target, scale):
-        for i in range(4):
-            low = sum(STAR[k] * XH[f, 0, 4 + i - k] for k in range(i + 1, 5))
-            high = sum(STAR[4 + m - i] * XH[f, 1, m] for m in range(i + 1))
-            target[i] = target[i] + scale(i) * low
-            target[12 + i] = target[12 + i] + scale(12 + i) * high
+    def add_x(f, target, scale, parts=((0, CY),)):
+        for start, stop in parts:
+            rows = slice(start, stop)
+            for i in range(4):
+                low = sum(STAR[k] * XH[f, 0, 4 + i - k, rows] for k in range(i + 1, 5))
+                high = sum(STAR[4 + m - i] * XH[f, 1, m, rows] for m in range(i + 1))
+                target[i, rows] = target[i, rows] + scale(i, rows) * low
+                target[12 + i, rows] = target[12 + i, rows] + scale(12 + i, rows) * high
 
     def near_y(f, x):
         at = 4 * x
@@ -311,10 +321,34 @@
         if sends:
             send_partial(s + 1, (1, 2))
         arrive(s, 0)
+        if s > 0:
+            each_side(0, lambda side: place(XM.at[s - 1, side], XH.at[s, side], ((0, 4), (1, 24))))
         add_x(s, target, step_scale)
         if sends:
+            send(s + 1, 0, slice(0, 1))
+            for side in range(2):
+                for t, row in ((0, 4), (1, 24)):
+                    for p in range(2):
+                        two = [target[12 * side + 2 * p + q, row : row + 4, :] for q in range(2)]
+                        XP[s, side, t, 8 * p : 8 * p + 8] = jnp.concatenate(two, axis=0)
+            send(s + 1, 0, slice(1, 3))
+        if s > 0:
+            arrive(s, 0, 3)
+            each_side(0, lambda side: place(XL.at[s - 1, side], XT.at[side], ((0, 0), (1, 12))))
+            for t, rows in ((0, slice(0, 8)), (1, slice(24, 32))):
+                own = slice(8 * t, 8 * t + 8)
+                for i in range(4):
+                    low = sum(STAR[k] * XT[0, 4 + i - k, own] for k in range(i + 1, 5))
+                    high = sum(STAR[4 + m - i] * XT[1, m, own] for m in range(i + 1))
+                    target[i, rows] = target[i, rows] + we[i, rows] * low
+                    target[12 + i, rows] = target[12 + i, rows] + we[12 + i, rows] * high
+        if sends:
             send_partial(s + 1, (0, 3))
-            send(s + 1, 0, slice(0, 1))
+
+    def place(packed, slabs, spots):
+        for t, row in spots:
+            for i in range(4):
+                slabs[i, row : row + 4] = packed[t, 4 * i : 4 * i + 4]
 
     def cross(f):
         for p in range(8):
@@ -344,11 +378,11 @@
                 highs.append(high[4:8])
                 target[x, 0:8] = low
                 target[x, 24:32] = high
-            if s < STEPS - 2:
+            if sends:
                 CP[s + 1, 0, 8 + 8 * p : 16 + 8 * p] = jnp.concatenate(lows, axis=0)
                 CP[s + 1, 1, 8 + 8 * p : 16 + 8 * p] = jnp.concatenate(highs, axis=0)
         if sends:
-            send(s + 1, 0, slice(1, 3))
+            send(s + 1, 0, slice(3, 5))
             pack_lanes(s + 1)
             send(s + 1, 2)
 
@@ -525,11 +559,14 @@
         vmem(shape, F32),
         vmem((8, 2, 4, CY, CZ), F32),
         vmem((9, 2, 64, CZ), F32), vmem((9, 2, 80, CZ), F32),
-        vmem((STEPS - 1, 2, 80, CZ), F32), vmem((2, 64, CZ), F32),
+        vmem((STEPS, 2, 80, CZ), F32), vmem((2, 64, CZ), F32),
+        vmem((STEPS - 1, 2, 2, 16, CZ), F32), vmem((STEPS - 1, 2, 2, 16, CZ), F32),
+        vmem((STEPS - 1, 2, 2, 16, CZ), F32), vmem((2, 4, 16, CZ), F32),
         vmem((8, 2, 16, CZ), F32), vmem((8, 2, 16, CZ), F32),
         pltpu.SemaphoreType.DMA((9,)),
         pltpu.SemaphoreType.DMA((3, 2)), pltpu.SemaphoreType.DMA((2, 2, 2)),
         pltpu.SemaphoreType.DMA((9, 2)), pltpu.SemaphoreType.DMA((STEPS, 2, 2)),
+        pltpu.SemaphoreType.DMA((2, 2)),
     ]
     vmem_spec = pl.BlockSpec(memory_space=pltpu.VMEM)
     hbm_spec = pl.BlockSpec(memory_space=pltpu.HBM)

time: 26.3 us -> 26.2 us (level)
  Pallas kernels: 25.6 us -> 25.2 us
    pallas_call x1, Pallas kernels: 24.7 us -> 24.3 us  [local(): pl.pallas_call(kernel, out_shape=(vmem(shape, F32),) * 3, in_specs=[hbm_s...]
where the time goes in v6:
time: 26.2 us; the launch traced here: 25.9 us
  Pallas kernels  25.2 us (96%)
  between operations  0.64 us (2%)
    pallas_call x1, Pallas kernels, local(): pl.pallas_call(kernel, out_shape=(vmem(shape, F32),) * 3, in_specs=[hbm_s...  24.3 us
    pallas_call x1, Pallas kernels, local(): pl.pallas_call(put_out, out_shape=(block,) * 3, in_specs=[pl.BlockSpec(me...  0.9 us

profile of v6, /device:TPU:24, one launch (start us, length us, event | category | flops | bytes accessed | tf_op | source)
XLA Modules:
  0.0 25.9 jit_solution(9150865561679057518)
XLA Ops:
  0.6 24.3 %adjoint_window.1 = (f32[16,32,128]{2,1,0:T(8,128)S(1)}, f32[16,32,128]{2,1,0:T(8,128)S(1)}, f32[16,32,128]{2,1,0:T(8,128)S(1)}) custom-call(f32[4,16,32,128]{3,2,1,0:T(8,128)} %coef.1, s32[4,4,8,32]{3,2,1,0:T(8,128)} %keep.1, f32[16,32,128]{2,1,0:T(8,128)} %cour.1, f32[16,32,128]{2,1,0:T(8,128)} %damp.1, f32[16,32,128]{2,1,0:T(8,128)} %nxt.1, ...), custom_call_target="tpu_custom_call" | custom-call | tf_op jit(solution)/shard_map/adjoint_window/pallas_call | solution.py:573
  25.0 0.9 %put_out.1 = (f32[16,32,128]{2,1,0:T(8,128)}, f32[16,32,128]{2,1,0:T(8,128)}, f32[16,32,128]{2,1,0:T(8,128)}) custom-call(f32[16,32,128]{2,1,0:T(8,128)S(1)} %get-tuple-element.6.grad_v, f32[16,32,128]{2,1,0:T(8,128)S(1)} %get-tuple-element.7.last_v, f32[16,32,128]{2,1,0:T(8,128)S(1)} %get-tuple-element.8.before_v), custom_call_target="tpu_custom_call" | custom-call | tf_op jit(solution)/shard_map/put_out/pallas_call | solution.py:588

commit v7 on v6

--- a/solution.py
+++ b/solution.py
@@ -434,8 +434,8 @@
         pack_rows(4 + s)
         pack_lanes(4 + s)
 
-    def post(s):
-        for d in (1, 0, 2):
+    def post(s, dims=(1, 0, 2)):
+        for d in dims:
             send(4 + s, d)
 
     for copy in edges:
@@ -495,10 +495,11 @@
     thr[...] = jnp.concatenate([dot(ops_v[672 + 256 * h : 928 + 256 * h, 0:CZ], wide) for h in range(2)]).reshape(STEPS, CX // 4, CY, CZ)
 
     prepare(0)
-    post(0)
+    post(0, (0, 2))
     adjoint_own(0)
     prepare(1)
     adjoint_near(0)
+    post(0, (1,))
     adjoint_rows(0)
     post(1)
     arrive(8, 1)

time: 26.2 us -> 26.5 us (1.011)
  the two profiles are of different devices: /device:TPU:24 before, /device:TPU:31 now
where the time goes in v7:
time: 26.5 us; the launch traced here: 26.4 us
  Pallas kernels  25.7 us (97%)
  between operations  0.64 us (2%)
    pallas_call x1, Pallas kernels, local(): pl.pallas_call(kernel, out_shape=(vmem(shape, F32),) * 3, in_specs=[hbm_s...  24.8 us
    pallas_call x1, Pallas kernels, local(): pl.pallas_call(put_out, out_shape=(block,) * 3, in_specs=[pl.BlockSpec(me...  0.9 us

profile of v7, /device:TPU:31, one launch (start us, length us, event | category | flops | bytes accessed | tf_op | source)
XLA Modules:
  0.0 26.4 jit_solution(5275499035068201105)
XLA Ops:
  0.6 24.8 %adjoint_window.1 = (f32[16,32,128]{2,1,0:T(8,128)S(1)}, f32[16,32,128]{2,1,0:T(8,128)S(1)}, f32[16,32,128]{2,1,0:T(8,128)S(1)}) custom-call(f32[4,16,32,128]{3,2,1,0:T(8,128)} %coef.1, s32[4,4,8,32]{3,2,1,0:T(8,128)} %keep.1, f32[16,32,128]{2,1,0:T(8,128)} %cour.1, f32[16,32,128]{2,1,0:T(8,128)} %damp.1, f32[16,32,128]{2,1,0:T(8,128)} %nxt.1, ...), custom_call_target="tpu_custom_call" | custom-call | tf_op jit(solution)/shard_map/adjoint_window/pallas_call | solution.py:574
  25.5 0.9 %put_out.1 = (f32[16,32,128]{2,1,0:T(8,128)}, f32[16,32,128]{2,1,0:T(8,128)}, f32[16,32,128]{2,1,0:T(8,128)}) custom-call(f32[16,32,128]{2,1,0:T(8,128)S(1)} %get-tuple-element.6.grad_v, f32[16,32,128]{2,1,0:T(8,128)S(1)} %get-tuple-element.7.last_v, f32[16,32,128]{2,1,0:T(8,128)S(1)} %get-tuple-element.8.before_v), custom_call_target="tpu_custom_call" | custom-call | tf_op jit(solution)/shard_map/put_out/pallas_call | solution.py:589
